TPU v7x, 128 devices: a 2x2x16 block of a 8x8x16 slice. The times are simulated.
128 devices in a mesh: grp: 4 (over y, x), row: 32 (over z, core).
Axes of the slice: x: 2, y: 2, z: 16, core: 2. Of those that a mesh axis runs over, the one named last changes fastest.
The devices are a block of a 8x8x16 slice.
Arguments:
- bin_index: int32 [262144, 10], P(('grp', 'row')), parts along dimension 0, may hold values from 0 to 32767, as said below
- pair_bin: int32 [262144, 45], P(('grp', 'row')), parts along dimension 0, may hold values from 0 to 5119, as said below
- predictor: float32 [262144], P(('grp', 'row')), parts along dimension 0, may hold values from -3 to 3
- response: float32 [262144], P(('grp', 'row')), parts along dimension 0, may hold values from 0 to 8
- marginal_basis: bfloat16 [10, 32768, 200], P(None, 'row'), may hold values from -0.1875 to 0.1875
- pair_left: int32 [45, 5120], P(None, 'row'), may hold values from 0 to 1023
- pair_right: int32 [45, 5120], P(None, 'row'), may hold values from 0 to 32767, as said below
- pair_terms: int32 [45, 2], replicated, may hold values from 0 to 9, as said below
Outputs:
- diag_blocks: float32 [40, 200, 200], P('grp'), parts along dimension 0
- cross_blocks: float32 [180, 200, 200], P('grp'), parts along dimension 0
- basis_response: float32 [40, 200], P('grp'), parts along dimension 0
There are 4 independent parts, one for each index of `grp`. A program takes and returns all parts, laid end to end along the dimension named above; an argument that names none is the same for every part. Nothing has to cross between parts.
Inputs may be any that keep to these rules, and one draw needn't show every extreme that they name: `bin_index`: row index o of the row axis holds bins o * 1024 to (o + 1) * 1024 - 1 of every covariate. Among the 2048 rows of one device, each column names bins held by any one index o at most 128 times, and exactly 128 times for some o in every column. `pair_bin`: row index o holds bin pairs o * 160 to (o + 1) * 160 - 1 of every term pair. Among the 2048 rows of one device, each column names bin pairs held by any one index o at most 128 times, and exactly 128 times for some o in every column. `pair_right`: bin pair c = o * 160 + s names a right bin held by row index s // 5, that is a bin between (s // 5) * 1024 and (s // 5 + 1) * 1024 - 1. `pair_terms`: each row holds two smooths l < r; every unordered pair of the 10 smooths stands in exactly one row.
All inputs are finite; a program needn't handle non-finite values.
Results may differ from a plain program's by a relative error of at most 0.0032.
Values may be sent and summed in bfloat16 or wider, within the bound.
No kernel may reach another device: no remote copies, remote signals or barrier semaphores. Data moves between devices by JAX's collectives and lax.ppermute only.
A program may use at most 192 MiB of HBM per device.

v0:
```python
import jax
import jax.numpy as jnp
from jax import lax
from jax.sharding import PartitionSpec as P


def cut_along(value, dim, count):
    shape = value.shape
    blocks = value.reshape(*shape[:dim], count, shape[dim] // count, *shape[dim + 1 :])
    return jnp.moveaxis(blocks, dim, 0)


def edges_of(length, count):
    unit = 8 if length >= 8 * count else 1
    return [length // unit * k // count * unit for k in range(1, count)]


def laid_out(blocks, dim):
    blocks = jnp.moveaxis(blocks, 0, dim)
    shape = blocks.shape
    return blocks.reshape(*shape[:dim], shape[dim] * shape[dim + 1], *shape[dim + 2 :])


def several_exchanges(value, axis, pieces, split_dim, concat_dim):
    blocks = cut_along(value, split_dim, lax.axis_size(axis))
    split_at = max(range(1, max(2, blocks.ndim - 1)), key=lambda d: blocks.shape[d])
    gathered = []
    for piece in jnp.split(blocks, edges_of(blocks.shape[split_at], pieces), axis=split_at):
        if piece.size:
            gathered.append(lax.all_to_all(piece, axis, split_axis=0, concat_axis=0, tiled=True))
    return laid_out(jnp.concatenate(gathered, axis=split_at), concat_dim)


def sum_packed(arrays, axis, dims):
    count = lax.axis_size(axis)
    blocks = [cut_along(a, dim, count) for a, dim in zip(arrays, dims)]
    lines = jnp.concatenate([b.reshape(count, -1) for b in blocks], axis=1)
    rows = max(16, -(-lines.shape[1] // 1024) * 8)
    lines = jnp.pad(lines, ((0, 0), (0, rows * 128 - lines.shape[1]))).reshape(-1, 128)
    line, at, gathered = (lax.psum_scatter(lines, axis, tiled=True).reshape(-1), 0, [])
    for b in blocks:
        part = b[0]
        gathered.append(line[at : at + part.size].reshape(part.shape))
        at += part.size
    return tuple(gathered)


def dense_sums(ids, per_owner, owners, channels):
    owner_range = jnp.arange(owners, dtype=jnp.int32)
    offset_range = jnp.arange(per_owner, dtype=jnp.int32)

    def column_table(column):
        owner_ids = column // per_owner
        offsets = column - owner_ids * per_owner
        owner_hot = (owner_ids[:, None] == owner_range[None, :]).astype(jnp.float32)
        stacked = jnp.concatenate([values[:, None] * owner_hot for values in channels], axis=1)
        offset_hot = (offsets[:, None] == offset_range[None, :]).astype(jnp.float32)
        table = jnp.dot(
            stacked.T,
            offset_hot,
            precision=lax.Precision.HIGHEST,
            preferred_element_type=jnp.float32,
        )
        return table.reshape(len(channels), owners * per_owner)

    tables = lax.map(column_table, jnp.transpose(ids))
    return jnp.transpose(tables, (1, 0, 2))


def on_device(
    bin_index, pair_bin, predictor, response, marginal_basis, pair_left, pair_right, pair_terms
):
    row_count = lax.axis_size("row")
    local_rows, cov_count = bin_index.shape
    bin_block = marginal_basis.shape[1]
    basis_width = marginal_basis.shape[2]
    pair_count, pair_block = pair_left.shape
    flat_basis = marginal_basis.reshape(cov_count * bin_block, basis_width)
    per_peer = pair_block // row_count
    right_offset = pair_right % bin_block
    requests = (pair_terms[:, 1][:, None] * bin_block + right_offset).reshape(
        pair_count, row_count, per_peer
    )
    found = jnp.take(
        flat_basis, lax.all_to_all(requests, "row", split_axis=1, concat_axis=1, tiled=True), axis=0
    )
    fetched = several_exchanges(found, "row", 2, 1, 1)
    right_rows = fetched.reshape(pair_count, pair_block, basis_width)
    rates = jnp.exp(predictor)
    working = rates * predictor + response - rates
    cov_table = dense_sums(bin_index, bin_block, row_count, (rates, working))
    pair_table = dense_sums(pair_bin, pair_block, row_count, (rates,))
    cov_sums, pair_sums = sum_packed((cov_table, pair_table), "row", (2, 2))
    weighted = (cov_sums[0][:, :, None] * marginal_basis).astype(jnp.bfloat16)
    diag_local = jnp.einsum(
        "jak,jal->jkl", weighted, marginal_basis, preferred_element_type=jnp.float32
    )
    side_local = jnp.einsum(
        "ja,jak->jk",
        cov_sums[1].astype(jnp.bfloat16),
        marginal_basis,
        preferred_element_type=jnp.float32,
    )
    left_rows = jnp.take(flat_basis, pair_terms[:, 0][:, None] * bin_block + pair_left, axis=0)
    weighted_left = (pair_sums[0][:, :, None] * left_rows).astype(jnp.bfloat16)
    cross_local = jnp.einsum(
        "pck,pcl->pkl", weighted_left, right_rows, preferred_element_type=jnp.float32
    )
    diag_blocks, cross_blocks, basis_response = lax.psum(
        (diag_local, cross_local, side_local), "row"
    )
    return (diag_blocks, cross_blocks, basis_response)


def solution(mesh):
    return jax.shard_map(
        on_device,
        mesh=mesh,
        in_specs=(
            P(("grp", "row"), None),
            P(("grp", "row"), None),
            P(("grp", "row")),
            P(("grp", "row")),
            P(None, "row", None),
            P(None, "row"),
            P(None, "row"),
            P(),
        ),
        out_specs=(P("grp", None, None), P("grp", None, None), P("grp", None)),
        check_vma=False,
    )
```

profile of v0, /device:TPU:69, one launch (start us, length us, event | category | flops | bytes accessed | tf_op | source)
XLA Modules:
  0.0 783.6 jit_solution(5595395567503309444)
XLA Ops:
  10.2 18.5 %all-to-all-start = ((s32[32,1,225]{2,1,0:T(1,128)}), s32[32,1,225]{2,1,0:T(1,128)S(1)}, u32[]{:S(2)}, u32[]{:S(2)}) async-start(s32[32,1,225]{2,1,0:T(1,128)} %reshape.207), calls=%async_computation.1 | async-start | bytes 65536 | tf_op jit(solution)/shard_map/all_to_all | solution.py:85
  29.5 154.8 %while.27 = (s32[]{:T(128)}, f32[45,1,5120]{2,1,0:T(1,128)}, s32[45,2048]{1,0:T(8,128)}, f32[2048]{0:T(1024)S(1)}, s32[]{:T(128)}) while((s32[]{:T(128)}, f32[45,1,5120]{2,1,0:T(1,128)}, s32[45,2048]{1,0:T(8,128)}, f32[2048]{0:T(1024)S(1)}, s32[]{:T(128)}) %tuple.83), condition=%wide.region_3.4_spmd.clone, body=%wide.region_2.3_spmd.clone.sunk | while | flops 126308352 | bytes 168013 | solution.py:66
  30.3 1.9 fusion.50
  33.8 1.9 fusion.50
  37.2 1.9 fusion.50
  40.6 1.9 fusion.50
  44.1 1.9 fusion.50
  47.5 1.9 fusion.50
  51.0 1.9 fusion.50
  54.4 1.9 fusion.50
  57.8 1.9 fusion.50
  61.3 1.9 fusion.50
  64.7 1.9 fusion.50
  68.2 1.9 fusion.50
  71.6 1.9 fusion.50
  75.0 1.9 fusion.50
  78.5 1.9 fusion.50
  81.9 1.9 fusion.50
  85.4 1.9 fusion.50
  88.8 1.9 fusion.50
  92.3 1.9 fusion.50
  99.1 1.9 fusion.50
  116.3 1.9 fusion.50
  126.7 1.9 fusion.50
  157.6 1.9 fusion.50
  181.7 1.9 fusion.50
  184.3 7.5 copy.22
  198.2 20.8 %gather_fusion.1 = bf16[7200,200]{1,0:T(8,128)(2,1)} fusion(bf16[10240,200]{1,0:T(8,128)(2,1)} %bitcast.43, s32[8192]{0:T(1024)S(1)} %pad_clamp_fusion), kind=kCustom, calls=%fused_computation.1 | custom fusion | bytes 5788800 | tf_op jit(solution)/shard_map/jit(_take)/gather | solution.py:84
  219.0 7.9 %gather.12 = bf16[45,32,1,5,200]{4,3,1,0,2:T(8,128)(2,1)} reshape(bf16[7200,200]{1,0:T(8,128)(2,1)} %gather_fusion.1) | data formatting | bytes 5760000 | tf_op jit(solution)/shard_map/jit(_take)/gather | solution.py:84
  226.9 5.1 select_bitcast_fusion
  232.0 2.6 copy-done
  234.8 2.2 copy.26
  237.0 12.4 %all-to-all-start.1 = ((bf16[32,16,1,5,200]{4,1,3,2,0:T(8,128)(2,1)}), bf16[32,16,1,5,200]{4,1,3,2,0:T(8,128)(2,1)}, u32[]{:S(2)}, u32[]{:S(2)}) async-start(bf16[32,16,1,5,200]{4,1,3,2,0:T(8,128)(2,1)} %copy.26), calls=%async_computation.2 | async-start | bytes 2621440 | tf_op jit(solution)/shard_map/all_to_all | solution.py:30
  249.4 55.6 %while.26 = (s32[]{:T(128)}, f32[10,2,32768]{2,1,0:T(2,128)S(1)}, s32[10,2048]{1,0:T(8,128)}, f32[2048]{0:T(1024)S(1)}, f32[2048]{0:T(1024)S(1)}, /*index=5*/s32[]{:T(128)}) while((s32[]{:T(128)}, f32[10,2,32768]{2,1,0:T(2,128)S(1)}, s32[10,2048]{1,0:T(8,128)}, f32[2048]{0:T(1024)S(1)}, f32[2048]{0:T(1024)S(1)}, ...), condition=%wide.region_1.2_spmd.clone, body=%wide.region_0.1_spmd.clone.sunk | while | flops 1613072384 | bytes 2433109 | solution.py:66
  251.2 3.5 fusion.48
  256.8 3.5 fusion.48
  262.3 3.5 fusion.48
  267.9 3.5 fusion.48
  273.4 3.5 fusion.48
  279.0 3.5 fusion.48
  284.6 3.5 fusion.48
  290.1 3.5 fusion.48
  295.7 3.5 fusion.48
  301.3 3.5 fusion.48
  306.5 3.4 reduce
  312.4 3.9 reshape.174
  316.3 3.6 copy.36
  319.9 2.5 reshape.175
  322.5 2.1 slice-done
  324.5 3.5 copy.27
  328.0 12.4 %all-to-all-start.2 = ((bf16[32,29,1,5,200]{4,1,3,2,0:T(8,128)(2,1)}), bf16[32,29,1,5,200]{4,1,3,2,0:T(8,128)(2,1)}, u32[]{:S(2)}, u32[]{:S(2)}) async-start(bf16[32,29,1,5,200]{4,1,3,2,0:T(8,128)(2,1)} %copy.27), calls=%async_computation.3 | async-start | bytes 5242880 | tf_op jit(solution)/shard_map/all_to_all | solution.py:30
  340.5 2.1 select_maximum_fusion
  342.6 3.6 reshape.177
  346.5 20.8 %gather_fusion = bf16[7200,200]{1,0:T(8,128)(2,1)} fusion(bf16[10240,200]{1,0:T(8,128)(2,1)} %bitcast.44, s32[8192]{0:T(1024)S(1)} %pad_clamp_fusion.1), kind=kCustom, calls=%fused_computation | custom fusion | bytes 5788800 | tf_op jit(solution)/shard_map/jit(_take)/gather | solution.py:104
  367.3 100.4 %all-to-all-done.2 = bf16[32,29,1,5,200]{4,1,3,2,0:T(8,128)(2,1)} async-done(((bf16[32,29,1,5,200]{4,1,3,2,0:T(8,128)(2,1)}), bf16[32,29,1,5,200]{4,1,3,2,0:T(8,128)(2,1)}, u32[]{:S(2)}, u32[]{:S(2)}) %all-to-all-start.2) | async-done | bytes 1856032 | tf_op jit(solution)/shard_map/all_to_all | solution.py:30
  467.7 4.8 pad_maximum_fusion
  472.5 36.9 %reduce-scatter.2.cloned.1.call-done = f32[224,128]{1,0:T(8,128)} async-done(((f32[7168,128]{1,0:T(8,128)}), f32[224,128]{1,0:T(8,128)}) %reduce-scatter.2.cloned.1.call-update) | async-done | bytes 114704 | tf_op jit(solution)/shard_map/reduce_scatter | solution.py:40
  511.1 6.2 fusion.26
  517.3 8.6 %fusion.28 = f32[45,200,200]{2,1,0:T(8,128)} fusion(bf16[45,160,200]{2,0,1:T(8,128)(2,1)S(1)} %bitcast.46, bf16[45,160,200]{2,1,0:T(8,128)(2,1)S(1)} %bitcast.47, f32[45,160]{1,0:T(8,128)S(1)} %mul.86, pred[45,160]{1,0:T(8,128)(4,1)S(1)} %get-tuple-element.217), kind=kOutput, calls=%fused_computation.49 | convolution fusion | flops 581760000 | bytes 12996000 | tf_op jit(solution)/shard_map/pck,pcl->pkl/dot_general | solution.py:106
  526.7 3.3 fusion.37
  530.1 90.3 %psum.23 = f32[10,200]{1,0:T(8,128)} all-reduce(f32[10,200]{1,0:T(8,128)S(1)} %bitcast.54), channel_id=1, replica_groups=mesh['grp'=4,'row'=32] {'row'}, use_global_device_ids=true, to_apply=%region_7.8 | all-reduce | flops 2000 | bytes 16000 | tf_op jit(solution)/shard_map/psum | solution.py:109
  620.4 145.5 %all-reduce.4.cloned.1.call-done = (f32[10,200,200]{2,1,0:T(8,128)}, f32[45,200,200]{2,1,0:T(8,128)}) async-done(((f32[10,200,200]{2,1,0:T(8,128)}, f32[45,200,200]{2,1,0:T(8,128)}), (f32[10,200,200]{2,1,0:T(8,128)}, f32[45,200,200]{2,1,0:T(8,128)})) %all-reduce.4.cloned.1.call-update) | async-done | bytes 8800016 | tf_op jit(solution)/shard_map/psum | solution.py:109
  765.9 3.0 copy.56
  768.9 7.9 %copy.57 = f32[45,200,200]{2,1,0:T(8,128)} copy(f32[45,200,200]{2,1,0:T(8,128)} %get-tuple-element.331) | data formatting | bytes 14400000
  (304 shorter events, 147.0 us)
Async XLA Ops:
  10.2 181.6 %all-to-all-start = ((s32[32,1,225]{2,1,0:T(1,128)}), s32[32,1,225]{2,1,0:T(1,128)S(1)}, u32[]{:S(2)}, u32[]{:S(2)}) async-start(s32[32,1,225]{2,1,0:T(1,128)} %reshape.207), calls=%async_computation.1 | async-start | bytes 65536 | tf_op jit(solution)/shard_map/all_to_all | solution.py:85
  184.3 7.5 copy-start.4
  232.0 2.6 copy-start
  234.8 14.7 %copy-start.5 = (f32[2048]{0:T(1024)S(1)}, f32[2048]{0:T(1024)}, u32[]{:S(2)}) copy-start(f32[2048]{0:T(1024)} %copy-done.4) | copy-start | bytes 24580
  237.0 91.0 %all-to-all-start.1 = ((bf16[32,16,1,5,200]{4,1,3,2,0:T(8,128)(2,1)}), bf16[32,16,1,5,200]{4,1,3,2,0:T(8,128)(2,1)}, u32[]{:S(2)}, u32[]{:S(2)}) async-start(bf16[32,16,1,5,200]{4,1,3,2,0:T(8,128)(2,1)} %copy.26), calls=%async_computation.2 | async-start | bytes 2621440 | tf_op jit(solution)/shard_map/all_to_all | solution.py:30
  305.1 1.5 copy-start.3
  322.4 2.1 slice-start
  328.0 139.7 %all-to-all-start.2 = ((bf16[32,29,1,5,200]{4,1,3,2,0:T(8,128)(2,1)}), bf16[32,29,1,5,200]{4,1,3,2,0:T(8,128)(2,1)}, u32[]{:S(2)}, u32[]{:S(2)}) async-start(bf16[32,29,1,5,200]{4,1,3,2,0:T(8,128)(2,1)} %copy.27), calls=%async_computation.3 | async-start | bytes 5242880 | tf_op jit(solution)/shard_map/all_to_all | solution.py:30
  340.4 169.0 %reduce-scatter.2.cloned.1.call-start = ((), (), s32[]{:S(2)}) async-start(), calls=%async_computation.4 | async-start | bytes 3784704 | tf_op jit(solution)/shard_map/reduce_scatter | solution.py:40
  342.6 3.7 copy-start.6
  342.6 3.7 copy-start.7
  346.2 419.7 %all-reduce.4.cloned.1.call-start = ((), (), s32[]{:S(2)}) async-start(), calls=%async_computation.5 | async-start | bytes 22528000 | tf_op jit(solution)/shard_map/psum | solution.py:109
  511.1 6.2 copy-start.1
  511.1 6.2 copy-start.2
Sparse Core Ops, SparseCore 0:
  346.3 163.0 reduce-scatter.1
  526.1 239.7 all-reduce.3
where the time goes:
time: 788 us; the launch traced here: 784 us
  waiting for transfers between devices  283 us (36%)
  local copies, waits for them, and re-layouts  185 us (23%)
  matrix products  137 us (17%)
  blocking collectives  90.3 us (11%)
  starting transfers between devices  43.5 us (6%)
  other arithmetic  30.1 us (4%)
  between operations  14.3 us (2%)
    psum x1, waiting for transfers between devices, on_device(): lax.psum((diag_local, cross_local, side_local), 'row')  145 us
    dot_general x55, matrix products, column_table(): jnp.dot(stacked.T, offset_hot, precision=lax.Precision.HIGHEST, preferred...  119 us
    all_to_all x2, waiting for transfers between devices, several_exchanges(): lax.all_to_all(piece, axis, split_axis=0, concat_axis=0, tiled=True)  100 us
    psum x1, blocking collectives, on_device(): lax.psum((diag_local, cross_local, side_local), 'row')  90.3 us
    dynamic_slice x55, local copies, waits for them, and re-layouts, dense_sums(): tables = lax.map(column_table, jnp.transpose(ids))  46.7 us
    reduce_scatter x1, waiting for transfers between devices, sum_packed(): lax.psum_scatter(lines, axis, tiled=True).reshape(-1)  36.9 us
    gather x2, local copies, waits for them, and re-layouts, on_device(): jnp.take(flat_basis, lax.all_to_all(requests, 'row', split_axis=1, concat...  28.7 us
    dynamic_update_slice x55, local copies, waits for them, and re-layouts, dense_sums(): tables = lax.map(column_table, jnp.transpose(ids))  27.8 us
  transfers between devices with their start and end apart: 5, of which 3 were waited for; matrix products, arithmetic and copies ran while one was open for 35% of the time, Pallas kernels for 0%

commit v1 on v0

v1 whole, which is shorter than its diff:
```python
import functools
import math

import jax
import jax.numpy as jnp
from jax import lax
from jax.experimental import pallas as pl
from jax.experimental.pallas import tpu as pltpu
from jax.sharding import PartitionSpec as P

LANES = 128
HALF = 64
UNIT = 40
VMEM_LIMIT = 60 * 1024 * 1024
f32, bf16, i32 = jnp.float32, jnp.bfloat16, jnp.int32
NT = (((1,), (1,)), ((), ()))
NN = (((1,), (0,)), ((), ()))


def up(value, step):
    return -(-value // step) * step


def dot(a, b, dims):
    return lax.dot_general(a, b, dims, preferred_element_type=f32)


def vmem():
    return pl.BlockSpec(memory_space=pltpu.VMEM)


def smem():
    return pl.BlockSpec(memory_space=pltpu.SMEM)


def params():
    return pltpu.CompilerParams(vmem_limit_bytes=VMEM_LIMIT)


def two_terms(value):
    high = value.astype(bf16)
    return high, (value - high.astype(f32)).astype(bf16)


class Plan:
    def __init__(self, devices, cluster, covs, width, bins, pairs, pair_block):
        self.devices, self.cluster = devices, cluster
        self.covs, self.width, self.bins = covs, width, bins
        self.pairs, self.pair_block = pairs, pair_block
        self.chips = devices // 2
        self.per = pair_block // devices
        self.own = -(-pairs // cluster)
        self.padded = self.own * cluster
        self.parts = bins // 256
        self.work_at = covs * bins // LANES
        self.pair_at = 2 * self.work_at
        self.rest = pair_block - LANES
        self.rest_fold = LANES // self.rest
        self.rest_at = self.pair_at + self.padded
        self.sum_rows = up(self.rest_at + -(-self.padded // self.rest_fold), 8)
        self.slot = up(self.per * self.own, 16)
        self.tails = -(-self.slot // HALF)
        self.packet = self.slot + self.slot // 2 + 8 * self.tails
        self.cuts = width // UNIT
        self.tail = width - LANES - HALF
        self.cross_blocks = self.blocks_of(self.own)
        self.diag_blocks = self.blocks_of(covs)
        self.cross_units = -(-self.cross_blocks * self.cuts // devices)
        self.diag_units = -(-self.diag_blocks * self.cuts // devices)
        self.diag_at = cluster * self.cross_units * UNIT
        self.share = self.diag_at + self.diag_units * UNIT

    def blocks_of(self, count):
        return count + -(-count // 2) + 1


def hist_kernel(plan, core_ref, bins_ref, pbins_ref, pred_ref, resp_ref, mine_ref, theirs_ref, iota_ref, own_ref, jo_ref):
    core = core_ref[0]
    rows = bins_ref.shape[1]
    iota_ref[...] = lax.broadcasted_iota(i32, iota_ref.shape, 0).astype(f32).astype(bf16)
    mine_ref[...] = jnp.zeros_like(mine_ref)
    theirs_ref[...] = jnp.zeros_like(theirs_ref)
    pred = pred_ref[...]
    rates = jnp.exp(pred)
    working = rates * pred + resp_ref[...] - rates
    rate_terms = two_terms(rates)
    work_terms = two_terms(working)
    chips, devices = plan.chips, plan.devices
    zero = jnp.zeros((), bf16)
    one = jnp.ones((), bf16)

    def place(owner):
        return ((owner & 1) ^ core) * chips + lax.shift_right_logical(owner, 1)

    def put(row, table):
        mine_ref[pl.ds(row, chips, stride=plan.sum_rows), :] = table[:chips]
        theirs_ref[pl.ds(row, chips, stride=plan.sum_rows), :] = table[chips:]

    pair_bins = pbins_ref[...]
    fifth = jnp.floor((pair_bins.astype(f32) + 0.5) * (1.0 / plan.per)).astype(i32)
    holder = lax.shift_right_logical(fifth, devices.bit_length() - 1)
    own_ref[...] = place(fifth & (devices - 1)).astype(f32).astype(bf16).astype(f32)
    jo_ref[...] = ((pair_bins - fifth * plan.per) * devices + holder).astype(f32)

    def pair_step(p, carry):
        own = own_ref[pl.ds(p, 1), :].astype(bf16)
        jo = jo_ref[pl.ds(p, 1), :].astype(bf16)
        own_hot = iota_ref[0:devices, :] == own
        left = jnp.concatenate([jnp.where(own_hot, t, zero) for t in rate_terms], axis=0)
        right = jnp.where(iota_ref[0 : plan.pair_block, :] == jo, one, zero)
        both = dot(left, right, NT)
        table = both[:devices] + both[devices:]
        put(plan.pair_at + p, table[:, :LANES])
        fold = plan.rest_fold
        line = plan.rest_at + p // fold
        at = (p % fold) * plan.rest
        lane = lax.broadcasted_iota(i32, (chips, LANES), 1)
        spread = jnp.concatenate([table[:, LANES:]] * fold, axis=1)
        keep = (lane >= at) & (lane < at + plan.rest)
        for ref, part in ((mine_ref, spread[:chips]), (theirs_ref, spread[chips:])):
            where = pl.ds(line, chips, stride=plan.sum_rows)
            ref[where, :] = jnp.where(keep, part, ref[where, :])
        return carry

    lax.fori_loop(0, plan.pairs, pair_step, 0)

    def cov_step(j, carry):
        ids = bins_ref[pl.ds(j, 1), :]
        owner = lax.shift_right_logical(ids, plan.bins.bit_length() - 1)
        offset = ids & (plan.bins - 1)
        spot = (lax.shift_right_logical(offset, 8) * devices + place(owner)).astype(f32).astype(bf16)
        low = (offset & 255).astype(f32).astype(bf16)
        spots = plan.parts * devices
        hot = iota_ref[0:spots, :] == spot
        left = jnp.concatenate([jnp.where(hot, t, zero) for t in rate_terms + work_terms], axis=0)
        right = jnp.where(iota_ref[0:256, :] == low, one, zero)
        both = dot(left, right, NT)
        for channel in range(2):
            base = 2 * channel * spots
            table = both[base : base + spots] + both[base + spots : base + 2 * spots]
            for part in range(plan.parts):
                for half in range(2):
                    put(
                        channel * plan.work_at + j * (plan.bins // LANES) + 2 * part + half,
                        table[part * devices : (part + 1) * devices, half * LANES : (half + 1) * LANES],
                    )
        return carry

    lax.fori_loop(0, plan.covs, cov_step, 0)


def histograms(plan, core, bins, pbins, pred, resp):
    rows = bins.shape[1]
    out = jax.ShapeDtypeStruct((plan.chips * plan.sum_rows, LANES), f32)
    tall = max(256, plan.parts * plan.devices, plan.pair_block)
    return pl.pallas_call(
        functools.partial(hist_kernel, plan),
        out_shape=(out, out),
        in_specs=[smem()] + [vmem()] * 4,
        out_specs=(vmem(), vmem()),
        scratch_shapes=[
            pltpu.VMEM((tall, rows), bf16),
            pltpu.VMEM(pbins.shape, f32),
            pltpu.VMEM(pbins.shape, f32),
        ],
        compiler_params=params(),
        name="histograms",
        cost_estimate=pl.CostEstimate(flops=12 * 10**9, bytes_accessed=8 * 10**6, transcendentals=rows),
    )(core, bins, pbins, pred, resp)


def pick_kernel(plan, terms_ref, left_ref, right_ref, basis_ref, out_ref, a_ref, b_ref):
    a_ref[...] = jnp.zeros_like(a_ref)
    b_ref[...] = jnp.zeros_like(b_ref)
    devices, slot = plan.devices, plan.slot
    count = plan.pair_block
    across = lax.broadcasted_iota(i32, (count, plan.bins), 1)
    lane = lax.broadcasted_iota(i32, (count, LANES), 1)
    extra = plan.width - LANES
    for i in range(plan.own):
        hot = (across == left_ref[:, i : i + 1]).astype(f32).astype(bf16)
        rows = dot(hot, basis_ref[terms_ref[i]], NT)
        right = right_ref[:, i : i + 1]
        high = lax.shift_right_logical(right, 5).astype(f32)
        low = (right & 31).astype(f32)
        end = jnp.concatenate([rows[:, LANES:], jnp.zeros((count, LANES - extra), f32)], axis=1)
        end = jnp.where(lane == extra, high, jnp.where(lane == extra + 1, low, end))
        for j in range(plan.per):
            where = pl.ds(j * plan.own + i, devices, stride=slot)
            a_ref[where, :] = rows[j * devices : (j + 1) * devices, :LANES]
            b_ref[where, :] = end[j * devices : (j + 1) * devices]

    def pack(q, carry):
        at = pl.multiple_of(q * slot, slot)
        a = a_ref[pl.ds(at, slot), :]
        b = b_ref[pl.ds(at, slot), :]
        half = slot // 2
        fold_lane = lax.broadcasted_iota(i32, (half, LANES), 1)
        folded = jnp.where(fold_lane < HALF, b[:half], pltpu.roll(b[half:], HALF, 1))
        tail_lane = lax.broadcasted_iota(i32, (8, LANES), 1)
        tails = []
        for n in range(plan.tails):
            tile = jnp.zeros((8, LANES), f32)
            for t in range(8):
                row = n * HALF + 8 * t
                if row >= slot:
                    break
                moved = pltpu.roll(b[row : row + 8], (16 * t - HALF) % LANES, 1)
                tile = jnp.where((tail_lane >= 16 * t) & (tail_lane < 16 * t + 16), moved, tile)
            tails.append(tile)
        out_ref[q] = jnp.concatenate([a, folded] + tails, axis=0).astype(bf16)
        return carry

    lax.fori_loop(0, devices, pack, 0)


def picked_rows(plan, terms, left, right, basis):
    return pl.pallas_call(
        functools.partial(pick_kernel, plan),
        out_shape=jax.ShapeDtypeStruct((plan.devices, plan.packet, LANES), bf16),
        in_specs=[smem()] + [vmem()] * 3,
        out_specs=vmem(),
        scratch_shapes=[pltpu.VMEM((plan.devices * plan.slot, LANES), f32)] * 2,
        compiler_params=params(),
        name="picked_rows",
        cost_estimate=pl.CostEstimate(flops=10**9, bytes_accessed=6 * 10**6, transcendentals=0),
    )(terms, left, right, basis)


def product_kernel(
    plan, core_ref, terms_ref, packet_ref, pair_w_ref, cov_w_ref, work_ref, basis_ref,
    mine_ref, theirs_ref, a_ref, b_ref, sums_ref,
):
    core = core_ref[0]
    devices, slot, chips = plan.devices, plan.slot, plan.chips
    width, own = plan.width, plan.own
    sums_ref[...] = jnp.zeros_like(sums_ref)
    half = slot // 2

    def unpack(o, carry):
        at = pl.multiple_of(o * slot, slot)
        y = packet_ref[o].astype(f32)
        a_ref[pl.ds(at, slot), :] = y[:slot]
        folded = y[slot : slot + half]
        turned = pltpu.roll(folded, HALF, 1)
        lane = lax.broadcasted_iota(i32, (8, LANES), 1)
        for n in range(plan.tails):
            tile = y[slot + half + 8 * n : slot + half + 8 * n + 8]
            for t in range(8):
                row = n * HALF + 8 * t
                if row >= slot:
                    break
                top = folded[row : row + 8] if row < half else turned[row - half : row - half + 8]
                moved = pltpu.roll(tile, (HALF - 16 * t) % LANES, 1)
                b_ref[pl.ds(at + row, 8), :] = jnp.where(lane < HALF, top, moved)
        return carry

    lax.fori_loop(0, devices, unpack, 0)

    def spot(block, cut, units, base):
        unit = block * plan.cuts + cut
        owner = unit // units
        place = ((owner & 1) ^ core) * chips + lax.shift_right_logical(owner, 1)
        return pl.multiple_of(place * plan.share + base + (unit % units) * UNIT, 8)

    def put(block, value, units, base, first=None, last=None):
        for cut in range(plan.cuts):
            where = pl.ds(spot(block, cut, units, base), UNIT)
            piece = value[cut * UNIT : (cut + 1) * UNIT]
            if first is None:
                sums_ref[where, :] = piece
            else:
                lane = lax.broadcasted_iota(i32, (UNIT, LANES), 1)
                keep = (lane >= first) & (lane < last)
                sums_ref[where, :] = jnp.where(keep, piece, sums_ref[where, :])

    def put_square(n, count, square, units, base):
        put(n, square[:, :LANES], units, base)
        rest = width - LANES
        side = jnp.concatenate([square[:, LANES:], jnp.zeros((width, LANES - rest), f32)], axis=1)
        at = (n % 2) * HALF
        put(count + n // 2, pltpu.roll(side, at, 1), units, base, at, at + HALF)
        tail_at = n * plan.tail
        put(
            count + -(-count // 2),
            pltpu.roll(side, (tail_at + HALF) % LANES, 1),
            units, base, tail_at, tail_at + plan.tail,
        )

    def diag_step(j, carry):
        basis = basis_ref[j]
        weighted = (basis.astype(f32) * cov_w_ref[pl.ds(j, 1), :]).astype(bf16)
        square = dot(weighted, basis, NT)
        put_square(j, plan.covs, square, plan.diag_units, plan.diag_at)
        side = dot(basis, work_ref[...], NT)
        column = lax.broadcasted_iota(i32, (width, LANES), 1)
        at = plan.covs * plan.tail
        put(
            plan.covs + -(-plan.covs // 2),
            pltpu.roll(side, at, 1),
            plan.diag_units, plan.diag_at, at + j, at + j + 1,
        )
        return carry

    lax.fori_loop(0, plan.covs, diag_step, 0)

    across = lax.broadcasted_iota(i32, (plan.pair_block, plan.bins), 1)
    extra = width - LANES

    def pair_step(i, carry):
        stride = [pl.ds(j * own + i, devices, stride=slot) for j in range(plan.per)]
        a = jnp.concatenate([a_ref[s, :] for s in stride], axis=0)
        b = jnp.concatenate([b_ref[s, :] for s in stride], axis=0)
        index = (b[:, extra : extra + 1] * 32.0 + b[:, extra + 1 : extra + 2]).astype(i32)
        hot = (across == index).astype(f32).astype(bf16)
        right = dot(hot, basis_ref[terms_ref[i]], NT).astype(bf16)
        left = jnp.concatenate([jnp.transpose(a), jnp.transpose(b)[:extra]], axis=0)
        for m in range(plan.cluster):
            weight = pair_w_ref[pl.ds(m * own + i, 1), :]
            square = dot((left * weight).astype(bf16), right, NN)
            put_square(i, own, square, plan.cross_units, m * plan.cross_units * UNIT)
        return carry

    lax.fori_loop(0, own, pair_step, 0)
    mine_ref[...] = sums_ref[: chips * plan.share, :]
    theirs_ref[...] = sums_ref[chips * plan.share :, :]


def products(plan, core, terms, packets, pair_w, cov_w, work, basis):
    out = jax.ShapeDtypeStruct((plan.chips * plan.share, LANES), f32)
    return pl.pallas_call(
        functools.partial(product_kernel, plan),
        out_shape=(out, out),
        in_specs=[smem(), smem()] + [vmem()] * 5,
        out_specs=(vmem(), vmem()),
        scratch_shapes=[pltpu.VMEM((plan.devices * plan.slot, LANES), f32)] * 2
        + [pltpu.VMEM((2 * plan.chips * plan.share, LANES), f32)],
        compiler_params=params(),
        name="products",
        cost_estimate=pl.CostEstimate(flops=4 * 10**9, bytes_accessed=26 * 10**6, transcendentals=0),
    )(core, terms, packets, pair_w, cov_w, work, basis)


def unpack_kernel(plan, own, count, units, base, in_ref, out_ref):
    p = pl.program_id(0)
    member, n = p // own, p % own
    start = base + member * units * UNIT

    def block(b):
        pieces = []
        for cut in range(plan.cuts):
            unit = b * plan.cuts + cut
            row = pl.multiple_of(start + (unit % units) * UNIT, 8)
            pieces.append(in_ref[unit // units, pl.ds(row, UNIT), :])
        return jnp.concatenate(pieces, axis=0).astype(f32)

    width = plan.width
    side = block(count + n // 2)
    tail = block(count + -(-count // 2))
    lane = lax.broadcasted_iota(i32, (width, LANES), 1)
    side = pltpu.roll(side, (n % 2) * HALF, 1)
    tail = pltpu.roll(tail, (HALF - n * plan.tail) % LANES, 1)
    out_ref[0, :, :LANES] = block(n)
    out_ref[0, :, LANES:] = jnp.where(lane < HALF, side, tail)[:, : width - LANES]


def unpacked(plan, total, own, count, units, base, lines):
    width = plan.width
    return pl.pallas_call(
        functools.partial(unpack_kernel, plan, own, count, units, base),
        out_shape=jax.ShapeDtypeStruct((total, width, width), f32),
        grid=(total,),
        in_specs=[vmem()],
        out_specs=pl.BlockSpec((1, width, width), lambda p: (p, 0, 0)),
        compiler_params=params(),
        name="unpacked",
        cost_estimate=pl.CostEstimate(flops=10**6, bytes_accessed=14 * 10**6, transcendentals=0),
    )(lines)


def clusters_of(groups):
    side = math.isqrt(groups)
    if side * side == groups and side % 2 == 0:
        return [
            [(y + b) * side + x + a for b in range(2) for a in range(2)]
            for y in range(0, side, 2)
            for x in range(0, side, 2)
        ]
    return [[g] for g in range(groups)]


def place_in(clusters, group):
    table = [0] * sum(len(c) for c in clusters)
    for members in clusters:
        for place, g in enumerate(members):
            table[g] = place
    return jnp.asarray(table, i32)[group]


def on_device(
    bin_index, pair_bin, predictor, response, marginal_basis, pair_left, pair_right, pair_terms
):
    devices, groups = lax.axis_size("row"), lax.axis_size("grp")
    clusters = clusters_of(groups)
    cluster = len(clusters[0])
    covs, bins, width = marginal_basis.shape
    pairs, pair_block = pair_left.shape
    plan = Plan(devices, cluster, covs, width, bins, pairs, pair_block)
    rings = [list(range(c, devices, 2)) for c in range(2)]
    swap = [(d, d ^ 1) for d in range(devices)]
    me = lax.axis_index("row")
    core = (me % 2).astype(i32).reshape(1)
    place = place_in(clusters, lax.axis_index("grp"))
    basis = jnp.swapaxes(marginal_basis, 1, 2)

    mine, theirs = histograms(
        plan, core, jnp.transpose(bin_index), jnp.transpose(pair_bin),
        predictor.reshape(1, -1), response.reshape(1, -1),
    )
    sums = mine + lax.ppermute(theirs, "row", swap)
    sums = lax.psum_scatter(sums, "row", axis_index_groups=rings, tiled=True)

    def my_pairs(table):
        padded = jnp.pad(table, ((0, plan.padded - pairs), (0, 0)))
        return lax.dynamic_slice(padded, (place * plan.own, 0), (plan.own, table.shape[1]))

    def columns(table):
        blocks = my_pairs(table).reshape(plan.own, devices, plan.per)
        return jnp.transpose(blocks, (2, 1, 0)).reshape(pair_block, plan.own)

    terms = my_pairs(pair_terms)
    packets = picked_rows(plan, terms[:, 0], columns(pair_left), columns(pair_right % bins), basis)
    packets = lax.all_to_all(packets, "row", split_axis=0, concat_axis=0, tiled=True)

    cov_w = sums[: plan.work_at].reshape(covs, bins)
    work = sums[plan.work_at : plan.pair_at].reshape(covs, bins).astype(bf16)
    work = jnp.pad(work, ((0, LANES - covs), (0, 0)))
    rest = sums[plan.rest_at : plan.rest_at + -(-plan.padded // plan.rest_fold)]
    pair_w = jnp.concatenate(
        [
            sums[plan.pair_at : plan.pair_at + plan.padded],
            rest.reshape(-1, plan.rest)[: plan.padded],
        ],
        axis=1,
    )
    if cluster > 1:
        pair_w = lax.all_to_all(
            pair_w.reshape(cluster, plan.own, pair_block), "grp", 0, 0,
            axis_index_groups=clusters, tiled=True,
        ).reshape(plan.padded, pair_block)

    mine, theirs = products(plan, core, terms[:, 1], packets, pair_w, cov_w, work, basis)
    total = mine + lax.ppermute(theirs, "row", swap)
    total = lax.psum_scatter(total, "row", axis_index_groups=rings, tiled=True)
    total = lax.optimization_barrier(total).astype(bf16)
    cross = total[: plan.diag_at]
    if cluster > 1:
        cross = lax.all_to_all(
            cross.reshape(cluster, -1, LANES), "grp", 0, 0, axis_index_groups=clusters, tiled=True
        ).reshape(plan.diag_at, LANES)
    share = jnp.concatenate([cross, total[plan.diag_at :]], axis=0)
    lines = lax.all_gather(share, "row", axis=0, tiled=True).reshape(devices, plan.share, LANES)

    cross_blocks = unpacked(plan, pairs, plan.own, plan.own, plan.cross_units, 0, lines)
    diag_blocks = unpacked(plan, covs, covs, covs, plan.diag_units, plan.diag_at, lines)
    side = []
    for cut in range(plan.cuts):
        unit = (plan.diag_blocks - 1) * plan.cuts + cut
        row = plan.diag_at + (unit % plan.diag_units) * UNIT
        side.append(lines[unit // plan.diag_units, row : row + UNIT])
    at = covs * plan.tail
    basis_response = jnp.transpose(jnp.concatenate(side, axis=0)[:, at : at + covs]).astype(f32)
    return diag_blocks, cross_blocks, basis_response


def solution(mesh):
    return jax.shard_map(
        on_device,
        mesh=mesh,
        in_specs=(
            P(("grp", "row"), None),
            P(("grp", "row"), None),
            P(("grp", "row")),
            P(("grp", "row")),
            P(None, "row", None),
            P(None, "row"),
            P(None, "row"),
            P(),
        ),
        out_specs=(P("grp", None, None), P("grp", None, None), P("grp", None)),
        check_vma=False,
    )
```

time: 788 us -> 426 us (0.54)
  local copies, waits for them, and re-layouts: 185 us -> 13.8 us
  matrix products: 137 us -> 0 us
  Pallas kernels: 0 us -> 95.7 us
  blocking collectives: 90.3 us -> 0 us
  waiting for transfers between devices: 283 us -> 254 us
  other arithmetic: 30.1 us -> 9.75 us
    psum x1 -> x0, waiting for transfers between devices: 145 us -> none  [on_device(): lax.psum((diag_local, cross_local, side_local), 'row')]
    dot_general x58 -> x0, matrix products: 137 us -> none  [the longest x55 119 us: column_table(): jnp.dot(stacked.T, offset_hot, precision=lax.Precision.HIGHEST, preferred...]
    pallas_call x0 -> x5, Pallas kernels: none -> 95.6 us  [the longest x1 31.9 us: histograms(): pl.pallas_call(functools.partial(hist_kernel, plan), out_shape=(out, out)...]
    psum x1 -> x0, blocking collectives: 90.3 us -> none  [on_device(): lax.psum((diag_local, cross_local, side_local), 'row')]
    all_gather x0 -> x1, waiting for transfers between devices: none -> 79.5 us  [on_device(): lax.all_gather(share, 'row', axis=0, tiled=True)]
    unnamed x2 -> x4, waiting for transfers between devices: 0.11 us -> 61.7 us
    all_to_all x3, waiting for transfers between devices: 100 us -> 47.4 us  [the longest x1 43.7 us: on_device(): lax.all_to_all(packets, 'row', split_axis=0, concat_axis=0, tiled=True)]
    gather x3 -> x0, local copies, waits for them, and re-layouts: 49.5 us -> none  [the longest x2 28.7 us: on_device(): jnp.take(flat_basis, lax.all_to_all(requests, 'row', split_axis=1, concat...]
  transfers between devices with their start and end apart: 5 -> 8, of which waited for: 3 -> 7; matrix products, arithmetic and copies ran while one was open for 35% -> 2% of each run, Pallas kernels for 0% -> 2%
where the time goes in v1:
time: 426 us; the launch traced here: 425 us
  waiting for transfers between devices  254 us (60%)
  Pallas kernels  95.7 us (22%)
  starting transfers between devices  37.8 us (9%)
  between operations  13.9 us (3%)
  local copies, waits for them, and re-layouts  13.8 us (3%)
  other arithmetic  9.75 us (2%)
    all_gather x1, waiting for transfers between devices, on_device(): lax.all_gather(share, 'row', axis=0, tiled=True)  79.5 us
    unnamed x4, waiting for transfers between devices  61.7 us
    reduce_scatter x1, waiting for transfers between devices, on_device(): sums = lax.psum_scatter(sums, 'row', axis_index_groups=rings, tiled=True)  53.8 us
    all_to_all x1, waiting for transfers between devices, on_device(): lax.all_to_all(packets, 'row', split_axis=0, concat_axis=0, tiled=True)  43.7 us
    pallas_call x1, Pallas kernels, histograms(): pl.pallas_call(functools.partial(hist_kernel, plan), out_shape=(out, out)...  31.9 us
    pallas_call x2, Pallas kernels, unpacked(): pl.pallas_call(functools.partial(unpack_kernel, plan, own, count, units,...  28.5 us
    pallas_call x1, Pallas kernels, products(): pl.pallas_call(functools.partial(product_kernel, plan), out_shape=(out, o...  26.2 us
    all_to_all x1, starting transfers between devices, on_device(): lax.all_to_all(packets, 'row', split_axis=0, concat_axis=0, tiled=True)  20.3 us
  transfers between devices with their start and end apart: 8, of which 7 were waited for; matrix products, arithmetic and copies ran while one was open for 2% of the time, Pallas kernels for 2%

profile of v1, /device:TPU:69, one launch (start us, length us, event | category | flops | bytes accessed | tf_op | source)
XLA Modules:
  0.0 424.9 jit_solution(2007191400282887341)
XLA Ops:
  7.2 0.1 reduce-scatter.5.cloned.1.call-start
  7.3 31.9 %histograms.1 = (f32[3584,128]{1,0:T(8,128)}, f32[3584,128]{1,0:T(8,128)}) custom-call(s32[1]{0:T(128)} %bitcast.core_ref, s32[10,2048]{1,0:T(8,128)} %bitcast.55, s32[45,2048]{1,0:T(8,128)} %bitcast.54, f32[1,2048]{1,0:T(1,128)} %bitcast.56, f32[1,2048]{1,0:T(1,128)} %bitcast.57), custom_call_target="tpu_custom_call" | custom-call | flops 12000000000 | bytes 8000000 | tf_op jit(solution)/shard_map/histograms/pallas_call | solution.py:156
  39.2 0.0 copy-start.2
  39.2 0.0 copy-start.3
  39.2 0.0 copy-start.4
  39.2 10.0 %collective-permute-start = (f32[3584,128]{1,0:T(8,128)}, f32[3584,128]{1,0:T(8,128)S(1)}, u32[]{:S(2)}, u32[]{:S(2)}) collective-permute-start(f32[3584,128]{1,0:T(8,128)} %get-tuple-element.8), channel_id=1, source_target_pairs={{0,1},{1,0},{2,3},{3,2},{4,5},{5,4},{6,7},{7,6},{8,9},{9,8},{10,11... | collective-permute-start | bytes 5505032 | tf_op jit(solution)/shard_map/ppermute | solution.py:420
  49.2 3.6 collective-permute-done
  52.8 3.0 add.40
  55.8 0.1 reduce-scatter.5.cloned.1.call-update
  55.9 0.0 copy-done.2
  55.9 0.0 copy-done.3
  55.9 0.2 reshape.54
  56.1 1.0 copy.17
  57.1 0.2 reshape.52
  57.3 1.0 copy.16
  58.3 0.0 copy-done.4
  58.3 0.1 pad_dynamic-slice_fusion.2
  58.4 0.6 slice_bitcast_fusion.5
  59.0 53.8 %reduce-scatter.5.cloned.1.call-done = f32[224,128]{1,0:T(8,128)} async-done(((f32[3584,128]{1,0:T(8,128)}), f32[224,128]{1,0:T(8,128)}) %reduce-scatter.5.cloned.1.call-update) | async-done | bytes 114704 | tf_op jit(solution)/shard_map/reduce_scatter | solution.py:421
  112.8 0.0 copy-start.1
  112.8 0.0 slice-start
  112.8 0.8 slice.58
  113.5 0.1 concatenate.15
  113.6 0.7 slice.57
  114.4 0.7 reshape.68
  115.1 3.4 all-to-all-start.1
  118.5 9.0 %picked_rows.1 = bf16[32,104,128]{2,1,0:T(8,128)(2,1)} custom-call(s32[12]{0:T(128)} %get-tuple-element.20.terms_ref, s32[160,12]{1,0:T(8,128)} %bitcast.53, s32[160,12]{1,0:T(8,128)} %bitcast.52, bf16[10,200,1024]{2,1,0:T(8,128)(2,1)} %bitcast.47), custom_call_target="tpu_custom_call" | custom-call | flops 1000000000 | bytes 6000000 | tf_op jit(solution)/shard_map/picked_rows/pallas_call | solution.py:218
  127.5 0.0 all-to-all-done.1
  127.5 20.3 %all-to-all-start = ((bf16[32,104,128]{2,1,0:T(8,128)(2,1)}), bf16[32,104,128]{2,1,0:T(8,128)(2,1)S(1)}, u32[]{:S(2)}, u32[]{:S(2)}) async-start(bf16[32,104,128]{2,1,0:T(8,128)(2,1)} %picked_rows.1), calls=%async_computation | async-start | bytes 1703936 | tf_op jit(solution)/shard_map/all_to_all | solution.py:433
  147.8 0.1 reduce-scatter.7.cloned.1.call-start
  147.9 0.0 copy-done.1
  147.9 0.0 slice-done
  147.9 0.6 reshape.59.cov_w_ref
  148.6 0.7 pad.18.work_ref
  149.3 0.5 broadcast.17
  149.8 0.7 reduce
  150.5 0.1 reshape.69
  150.6 0.6 reshape.58.pair_w_ref
  151.3 43.7 %all-to-all-done.packet_ref = bf16[32,104,128]{2,1,0:T(8,128)(2,1)S(1)} async-done(((bf16[32,104,128]{2,1,0:T(8,128)(2,1)}), bf16[32,104,128]{2,1,0:T(8,128)(2,1)S(1)}, u32[]{:S(2)}, u32[]{:S(2)}) %all-to-all-start) | async-done | bytes 852000 | tf_op jit(solution)/shard_map/all_to_all | solution.py:433
  194.9 0.0 copy-start
  194.9 0.9 copy-done
  195.8 26.2 %products.1 = (f32[9600,128]{1,0:T(8,128)}, f32[9600,128]{1,0:T(8,128)}) custom-call(s32[1]{0:T(128)} %bitcast.core_ref, s32[12]{0:T(128)} %get-tuple-element.21.terms_ref, bf16[32,104,128]{2,1,0:T(8,128)(2,1)} %copy-done, f32[48,160]{1,0:T(8,128)} %reshape.58.pair_w_ref, f32[10,1024]{1,0:T(8,128)} %reshape.59.cov_w_ref, bf16[128,1024]{1,0:T(8,128)(2,1)} %pad.18.work_ref, ...), custom_call_target="tpu_custom_call" | custom-call | flops 4000000000 | bytes 26000000 | tf_op jit(solution)/shard_map/products/pallas_call | solution.py:331
  222.0 0.5 collective-permute-start.1
  222.6 8.0 %collective-permute-done.1 = f32[9600,128]{1,0:T(8,128)S(1)} collective-permute-done((f32[9600,128]{1,0:T(8,128)}, f32[9600,128]{1,0:T(8,128)S(1)}, u32[]{:S(2)}, u32[]{:S(2)}) %collective-permute-start.1) | collective-permute-done | bytes 4915232 | tf_op jit(solution)/shard_map/ppermute | solution.py:453
  230.6 4.3 %add.41 = f32[9600,128]{1,0:T(8,128)} add(f32[9600,128]{1,0:T(8,128)} %get-tuple-element.9, f32[9600,128]{1,0:T(8,128)S(1)} %collective-permute-done.1) | non-fusion elementwise | flops 1228800 | bytes 14745600 | tf_op jit(solution)/shard_map/add | solution.py:453
  234.9 0.1 reduce-scatter.7.cloned.1.call-update
  234.9 61.5 %reduce-scatter.7.cloned.1.call-done = f32[600,128]{1,0:T(8,128)} async-done(((f32[9600,128]{1,0:T(8,128)}), f32[600,128]{1,0:T(8,128)}) %reduce-scatter.7.cloned.1.call-update) | async-done | bytes 307216
  296.5 1.0 convert_element_type.16
  297.4 0.7 slice.61
  298.1 3.4 all-to-all-start.2
  301.5 0.1 all-gather.2.cloned.1.call-start
  301.6 3.7 all-to-all-done.2
  305.3 0.7 pad_maximum_fusion
  306.0 0.1 all-gather.2.cloned.1.call-update
  306.0 79.5 %all-gather.2.cloned.1.call-done = bf16[19200,128]{1,0:T(8,128)(2,1)} async-done(((bf16[600,128]{1,0:T(8,128)(2,1)}), bf16[19200,128]{1,0:T(8,128)(2,1)}) %all-gather.2.cloned.1.call-update) | async-done | bytes 4915216 | tf_op jit(solution)/shard_map/all_gather | solution.py:462
  385.5 0.7 constant_dynamic-update-slice_fusion.4
  386.2 6.8 %unpacked.2 = f32[10,200,200]{2,1,0:T(8,128)} custom-call(bf16[32,600,128]{2,1,0:T(8,128)(2,1)} %bitcast.41), custom_call_target="tpu_custom_call" | custom-call | flops 1000000 | bytes 14000000 | tf_op jit(solution)/shard_map/unpacked/pallas_call | solution.py:369
  393.0 21.7 %unpacked.3 = f32[45,200,200]{2,1,0:T(8,128)} custom-call(bf16[32,600,128]{2,1,0:T(8,128)(2,1)} %bitcast.42), custom_call_target="tpu_custom_call" | custom-call | flops 1000000 | bytes 14000000 | tf_op jit(solution)/shard_map/unpacked/pallas_call | solution.py:369
  414.8 0.7 constant_dynamic-update-slice_fusion.3
  415.5 0.7 constant_dynamic-update-slice_fusion.2
  416.2 0.7 constant_dynamic-update-slice_fusion.1
  416.9 0.7 constant_dynamic-update-slice_fusion
  417.6 0.1 convert_bitcast_fusion
  417.7 0.7 copy.18
  (7 shorter events, 0.1 us)
Async XLA Ops:
  7.2 105.6 %reduce-scatter.5.cloned.1.call-start = ((), (), s32[]{:S(2)}) async-start(), calls=%async_computation.5 | async-start | bytes 1949696 | tf_op jit(solution)/shard_map/reduce_scatter | solution.py:421
  39.2 16.7 %copy-start.2 = (s32[45,160]{1,0:T(8,128)S(1)}, s32[45,160]{1,0:T(8,128)}, u32[]{:S(2)}) copy-start(s32[45,160]{1,0:T(8,128)} %param.15) | copy-start | bytes 86404
  39.2 16.7 %copy-start.3 = (s32[45,160]{1,0:T(8,128)S(1)}, s32[45,160]{1,0:T(8,128)}, u32[]{:S(2)}) copy-start(s32[45,160]{1,0:T(8,128)} %param.14) | copy-start | bytes 86404
  39.2 19.1 %copy-start.4 = (s32[45,2]{0,1:T(2,128)S(1)}, s32[45,2]{0,1:T(2,128)}, u32[]{:S(2)}) copy-start(s32[45,2]{0,1:T(2,128)} %param.16) | copy-start | bytes 1084
  39.2 13.6 %collective-permute-start = (f32[3584,128]{1,0:T(8,128)}, f32[3584,128]{1,0:T(8,128)S(1)}, u32[]{:S(2)}, u32[]{:S(2)}) collective-permute-start(f32[3584,128]{1,0:T(8,128)} %get-tuple-element.8), channel_id=1, source_target_pairs={{0,1},{1,0},{2,3},{3,2},{4,5},{5,4},{6,7},{7,6},{8,9},{9,8},{10,11... | collective-permute-start | bytes 5505032 | tf_op jit(solution)/shard_map/ppermute | solution.py:420
  112.8 35.1 %copy-start.1 = (f32[224,128]{1,0:T(8,128)S(1)}, f32[224,128]{1,0:T(8,128)}, u32[]{:S(2)}) copy-start(f32[224,128]{1,0:T(8,128)} %reduce-scatter.5.cloned.1.call-done) | copy-start | bytes 344068
  112.8 35.1 %slice-start = ((f32[224,128]{1,0:T(8,128)}), f32[80,128]{1,0:T(8,128)S(1)}, s32[]{:S(2)}) async-start(f32[224,128]{1,0:T(8,128)} %reduce-scatter.5.cloned.1.call-done), calls=%async_computation.8 | async-start | bytes 81920 | tf_op jit(solution)/shard_map/slice | solution.py:435
  115.1 12.4 %all-to-all-start.1 = ((f32[4,1,1920]{2,1,0:T(1,128)}), f32[4,1,1920]{2,1,0:T(1,128)S(1)}, u32[]{:S(2)}, u32[]{:S(2)}) async-start(f32[4,1,1920]{2,1,0:T(1,128)} %reshape.68), calls=%async_computation.2 | async-start | bytes 61440 | tf_op jit(solution)/shard_map/all_to_all | solution.py:447
  127.5 67.4 %all-to-all-start = ((bf16[32,104,128]{2,1,0:T(8,128)(2,1)}), bf16[32,104,128]{2,1,0:T(8,128)(2,1)S(1)}, u32[]{:S(2)}, u32[]{:S(2)}) async-start(bf16[32,104,128]{2,1,0:T(8,128)(2,1)} %picked_rows.1), calls=%async_computation | async-start | bytes 1703936 | tf_op jit(solution)/shard_map/all_to_all | solution.py:433
  147.8 148.7 %reduce-scatter.7.cloned.1.call-start = ((), (), s32[]{:S(2)}) async-start(), calls=%async_computation.7 | async-start | bytes 5222400
  194.9 0.9 copy-start
  222.0 8.6 %collective-permute-start.1 = (f32[9600,128]{1,0:T(8,128)}, f32[9600,128]{1,0:T(8,128)S(1)}, u32[]{:S(2)}, u32[]{:S(2)}) collective-permute-start(f32[9600,128]{1,0:T(8,128)} %get-tuple-element.10), channel_id=1, source_target_pairs={{0,1},{1,0},{2,3},{3,2},{4,5},{5,4},{6,7},{7,6},{8,9},{9,8},{10,11... | collective-permute-start | bytes 14745608 | tf_op jit(solution)/shard_map/ppermute | solution.py:453
  298.1 7.2 %all-to-all-start.2 = ((bf16[4,120,128]{2,1,0:T(8,128)(2,1)}), bf16[4,120,128]{2,1,0:T(8,128)(2,1)S(1)}, u32[]{:S(2)}, u32[]{:S(2)}) async-start(bf16[4,120,128]{2,1,0:T(8,128)(2,1)} %bitcast.13), calls=%async_computation.3 | async-start | bytes 245760 | tf_op jit(solution)/shard_map/all_to_all | solution.py:458
  301.5 84.0 %all-gather.2.cloned.1.call-start = ((), (), s32[]{:S(2)}) async-start(), calls=%async_computation.6 | async-start | bytes 5068800 | tf_op jit(solution)/shard_map/all_gather | solution.py:462
Sparse Core Ops, SparseCore 0:
  56.0 56.7 reduce-scatter.4
  235.1 61.3 reduce-scatter.6
  306.1 79.3 all-gather.1

commit v2 on v1

--- a/solution.py
+++ b/solution.py
@@ -56,8 +56,8 @@
         self.pair_at = 2 * self.work_at
         self.rest = pair_block - LANES
         self.rest_fold = LANES // self.rest
-        self.rest_at = self.pair_at + self.padded
-        self.sum_rows = up(self.rest_at + -(-self.padded // self.rest_fold), 8)
+        self.member = up(self.own + -(-self.own // self.rest_fold), 8)
+        self.sum_rows = up(self.pair_at + self.cluster * self.member, 8)
         self.slot = up(self.per * self.own, 16)
         self.tails = -(-self.slot // HALF)
         self.packet = self.slot + self.slot // 2 + 8 * self.tails
@@ -69,6 +69,9 @@
         self.diag_units = -(-self.diag_blocks * self.cuts // devices)
         self.diag_at = cluster * self.cross_units * UNIT
         self.share = self.diag_at + self.diag_units * UNIT
+        self.starts = [m * self.cross_units * UNIT for m in range(cluster)] + [self.diag_at]
+        self.counts = [self.cross_units * UNIT] * cluster + [self.diag_units * UNIT]
+        self.chunk = up(max(c + c // UNIT for c in self.counts), 16)
 
     def blocks_of(self, count):
         return count + -(-count // 2) + 1
@@ -96,33 +99,39 @@
         mine_ref[pl.ds(row, chips, stride=plan.sum_rows), :] = table[:chips]
         theirs_ref[pl.ds(row, chips, stride=plan.sum_rows), :] = table[chips:]
 
+    middle = plan.pair_block // 2
     pair_bins = pbins_ref[...]
     fifth = jnp.floor((pair_bins.astype(f32) + 0.5) * (1.0 / plan.per)).astype(i32)
     holder = lax.shift_right_logical(fifth, devices.bit_length() - 1)
-    own_ref[...] = place(fifth & (devices - 1)).astype(f32).astype(bf16).astype(f32)
-    jo_ref[...] = ((pair_bins - fifth * plan.per) * devices + holder).astype(f32)
+    within = (pair_bins - fifth * plan.per) * devices + holder
+    late = (within >= middle).astype(i32)
+    own_ref[...] = (place(fifth & (devices - 1)) + late * devices).astype(f32)
+    jo_ref[...] = (within - late * middle).astype(f32)
 
     def pair_step(p, carry):
         own = own_ref[pl.ds(p, 1), :].astype(bf16)
         jo = jo_ref[pl.ds(p, 1), :].astype(bf16)
-        own_hot = iota_ref[0:devices, :] == own
+        own_hot = iota_ref[0 : 2 * devices, :] == own
         left = jnp.concatenate([jnp.where(own_hot, t, zero) for t in rate_terms], axis=0)
-        right = jnp.where(iota_ref[0 : plan.pair_block, :] == jo, one, zero)
+        right = jnp.where(iota_ref[0:middle, :] == jo, one, zero)
         both = dot(left, right, NT)
-        table = both[:devices] + both[devices:]
-        put(plan.pair_at + p, table[:, :LANES])
-        fold = plan.rest_fold
-        line = plan.rest_at + p // fold
-        at = (p % fold) * plan.rest
-        lane = lax.broadcasted_iota(i32, (chips, LANES), 1)
-        spread = jnp.concatenate([table[:, LANES:]] * fold, axis=1)
-        keep = (lane >= at) & (lane < at + plan.rest)
-        for ref, part in ((mine_ref, spread[:chips]), (theirs_ref, spread[chips:])):
+        table = both[: 2 * devices] + both[2 * devices :]
+        table = jnp.concatenate([table, jnp.zeros((2 * devices, LANES - middle), f32)], axis=1)
+        lane = lax.broadcasted_iota(i32, (devices, LANES), 1)
+        second = table[devices:]
+        first_line = plan.pair_at + (p // plan.own) * plan.member
+        n = p % plan.own
+        put(first_line + n, jnp.where(lane < middle, table[:devices], pltpu.roll(second, middle, 1)))
+        line = first_line + plan.own + n // plan.rest_fold
+        at = (n % plan.rest_fold) * plan.rest
+        moved = pltpu.roll(second, (at + middle) % LANES, 1)
+        keep = (lane[:chips] >= at) & (lane[:chips] < at + plan.rest)
+        for ref, part in ((mine_ref, moved[:chips]), (theirs_ref, moved[chips:])):
             where = pl.ds(line, chips, stride=plan.sum_rows)
             ref[where, :] = jnp.where(keep, part, ref[where, :])
         return carry
 
-    lax.fori_loop(0, plan.pairs, pair_step, 0)
+    lax.fori_loop(0, plan.pairs, pair_step, 0, unroll=3)
 
     def cov_step(j, carry):
         ids = bins_ref[pl.ds(j, 1), :]
@@ -146,13 +155,13 @@
                     )
         return carry
 
-    lax.fori_loop(0, plan.covs, cov_step, 0)
+    lax.fori_loop(0, plan.covs, cov_step, 0, unroll=2)
 
 
 def histograms(plan, core, bins, pbins, pred, resp):
     rows = bins.shape[1]
     out = jax.ShapeDtypeStruct((plan.chips * plan.sum_rows, LANES), f32)
-    tall = max(256, plan.parts * plan.devices, plan.pair_block)
+    tall = max(256, plan.parts * plan.devices)
     return pl.pallas_call(
         functools.partial(hist_kernel, plan),
         out_shape=(out, out),
@@ -228,13 +237,12 @@
 
 
 def product_kernel(
-    plan, core_ref, terms_ref, packet_ref, pair_w_ref, cov_w_ref, work_ref, basis_ref,
-    mine_ref, theirs_ref, a_ref, b_ref, sums_ref,
+    plan, core_ref, terms_ref, packet_ref, pair_w_ref, weights_ref, basis_ref,
+    mine_ref, theirs_ref, a_ref, b_ref, work_ref, sums_ref,
 ):
     core = core_ref[0]
     devices, slot, chips = plan.devices, plan.slot, plan.chips
     width, own = plan.width, plan.own
-    sums_ref[...] = jnp.zeros_like(sums_ref)
     half = slot // 2
 
     def unpack(o, carry):
@@ -287,22 +295,45 @@
             units, base, tail_at, tail_at + plan.tail,
         )
 
-    def diag_step(j, carry):
+    def clear(count, units, base):
+        blocks = plan.blocks_of(count)
+        parts = [(blocks - 1) * plan.cuts + c for c in range(plan.cuts)]
+        parts += list(range(blocks * plan.cuts, units * devices))
+        if count % 2:
+            parts += [(blocks - 2) * plan.cuts + c for c in range(plan.cuts)]
+        for unit in parts:
+            where = pl.ds(spot(unit // plan.cuts, unit % plan.cuts, units, base), UNIT)
+            sums_ref[where, :] = jnp.zeros((UNIT, LANES), f32)
+
+    for m in range(plan.cluster):
+        clear(own, plan.cross_units, m * plan.cross_units * UNIT)
+    clear(plan.covs, plan.diag_units, plan.diag_at)
+
+    lines = plan.bins // LANES
+    work_ref[...] = jnp.zeros_like(work_ref)
+    for j in range(plan.covs):
+        for t in range(lines):
+            row = plan.work_at + j * lines + t
+            work_ref[j : j + 1, t * LANES : (t + 1) * LANES] = weights_ref[row : row + 1, :]
+    work = work_ref[...].astype(bf16)
+    column = lax.broadcasted_iota(i32, (width, work_ref.shape[0]), 1)
+
+    def diag_step(j, side):
         basis = basis_ref[j]
-        weighted = (basis.astype(f32) * cov_w_ref[pl.ds(j, 1), :]).astype(bf16)
+        rows = weights_ref[pl.ds(pl.multiple_of(j * lines, lines), lines), :]
+        weight = jnp.concatenate([rows[t : t + 1] for t in range(lines)], axis=1)
+        weighted = (basis.astype(f32) * weight).astype(bf16)
         square = dot(weighted, basis, NT)
         put_square(j, plan.covs, square, plan.diag_units, plan.diag_at)
-        side = dot(basis, work_ref[...], NT)
-        column = lax.broadcasted_iota(i32, (width, LANES), 1)
-        at = plan.covs * plan.tail
-        put(
-            plan.covs + -(-plan.covs // 2),
-            pltpu.roll(side, at, 1),
-            plan.diag_units, plan.diag_at, at + j, at + j + 1,
-        )
-        return carry
-
-    lax.fori_loop(0, plan.covs, diag_step, 0)
+        return jnp.where(column == j, dot(basis, work, NT), side)
+
+    side = lax.fori_loop(0, plan.covs, diag_step, jnp.zeros(column.shape, f32))
+    at = plan.covs * plan.tail
+    side = jnp.concatenate([side, jnp.zeros((width, LANES - side.shape[1]), f32)], axis=1)
+    put(
+        plan.diag_blocks - 1, pltpu.roll(side, at, 1),
+        plan.diag_units, plan.diag_at, at, at + plan.covs,
+    )
 
     across = lax.broadcasted_iota(i32, (plan.pair_block, plan.bins), 1)
     extra = width - LANES
@@ -316,7 +347,11 @@
         right = dot(hot, basis_ref[terms_ref[i]], NT).astype(bf16)
         left = jnp.concatenate([jnp.transpose(a), jnp.transpose(b)[:extra]], axis=0)
         for m in range(plan.cluster):
-            weight = pair_w_ref[pl.ds(m * own + i, 1), :]
+            start = m * plan.member
+            turn = (LANES - (i % plan.rest_fold) * plan.rest) % LANES
+            rest = pair_w_ref[pl.ds(start + own + i // plan.rest_fold, 1), :]
+            rest = pltpu.roll(jnp.broadcast_to(rest, (8, LANES)), turn, 1)[:1, : plan.rest]
+            weight = jnp.concatenate([pair_w_ref[pl.ds(start + i, 1), :], rest], axis=1)
             square = dot((left * weight).astype(bf16), right, NN)
             put_square(i, own, square, plan.cross_units, m * plan.cross_units * UNIT)
         return carry
@@ -326,56 +361,130 @@
     theirs_ref[...] = sums_ref[chips * plan.share :, :]
 
 
-def products(plan, core, terms, packets, pair_w, cov_w, work, basis):
+def products(plan, core, terms, packets, pair_w, weights, basis):
     out = jax.ShapeDtypeStruct((plan.chips * plan.share, LANES), f32)
     return pl.pallas_call(
         functools.partial(product_kernel, plan),
         out_shape=(out, out),
-        in_specs=[smem(), smem()] + [vmem()] * 5,
+        in_specs=[smem(), smem()] + [vmem()] * 4,
         out_specs=(vmem(), vmem()),
         scratch_shapes=[pltpu.VMEM((plan.devices * plan.slot, LANES), f32)] * 2
-        + [pltpu.VMEM((2 * plan.chips * plan.share, LANES), f32)],
+        + [
+            pltpu.VMEM((up(plan.covs, 16), plan.bins), f32),
+            pltpu.VMEM((2 * plan.chips * plan.share, LANES), f32),
+        ],
         compiler_params=params(),
         name="products",
         cost_estimate=pl.CostEstimate(flops=4 * 10**9, bytes_accessed=26 * 10**6, transcendentals=0),
-    )(core, terms, packets, pair_w, cov_w, work, basis)
-
-
-def unpack_kernel(plan, own, count, units, base, in_ref, out_ref):
-    p = pl.program_id(0)
-    member, n = p // own, p % own
-    start = base + member * units * UNIT
-
-    def block(b):
+    )(core, terms, packets, pair_w, weights, basis)
+
+
+def pack_kernel(plan, in_ref, out_ref):
+    for k, (start, count) in enumerate(zip(plan.starts, plan.counts)):
+        rows, steps = [], []
+        for at in range(start, start + count, UNIT):
+            part = in_ref[at : at + UNIT, :]
+            top = jnp.max(jnp.max(jnp.abs(part), axis=0, keepdims=True), axis=1, keepdims=True)
+            step = jnp.ceil(jnp.log2(jnp.maximum(top, 1e-30)) - 14.98)
+            rows.append(jnp.round(part * jnp.exp2(-step)))
+            steps.append(jnp.broadcast_to(step, (1, LANES)))
+        steps.append(jnp.zeros((plan.chunk - count - len(steps), LANES), f32))
+        out_ref[k] = jnp.concatenate(rows + steps, axis=0).astype(i32).astype(jnp.int16)
+
+
+def packed(plan, share):
+    return pl.pallas_call(
+        functools.partial(pack_kernel, plan),
+        out_shape=jax.ShapeDtypeStruct((plan.cluster + 1, plan.chunk, LANES), jnp.int16),
+        in_specs=[vmem()],
+        out_specs=vmem(),
+        compiler_params=params(),
+        name="packed",
+        cost_estimate=pl.CostEstimate(flops=10**6, bytes_accessed=5 * 10**5, transcendentals=16),
+    )(share)
+
+
+def unpack_kernel(plan, each, core_ref, mine_ref, theirs_ref, cross_ref, diag_ref, side_ref, sums_ref):
+    turn = pl.program_id(0)
+    core = core_ref[0]
+    width, covs = plan.width, plan.covs
+
+    @pl.when(turn == 0)
+    def _():
+        def chip(z, carry):
+            for ref, owner in ((mine_ref, 2 * z + core), (theirs_ref, 2 * z + 1 - core)):
+                for k, (start, count) in enumerate(zip(plan.starts, plan.counts)):
+                    part = ref[z, k * plan.chunk : (k + 1) * plan.chunk, :].astype(i32).astype(f32)
+                    steps = jnp.exp2(part[count:])
+                    for u in range(count // UNIT):
+                        at = u * UNIT
+                        sums_ref[owner, start + at : start + at + UNIT, :] = (
+                            part[at : at + UNIT] * steps[u : u + 1]
+                        )
+            return carry
+
+        lax.fori_loop(0, plan.chips, chip, 0)
+
+    def block(b, units, base):
         pieces = []
         for cut in range(plan.cuts):
             unit = b * plan.cuts + cut
-            row = pl.multiple_of(start + (unit % units) * UNIT, 8)
-            pieces.append(in_ref[unit // units, pl.ds(row, UNIT), :])
-        return jnp.concatenate(pieces, axis=0).astype(f32)
-
-    width = plan.width
-    side = block(count + n // 2)
-    tail = block(count + -(-count // 2))
+            row = pl.multiple_of(base + (unit % units) * UNIT, 8)
+            pieces.append(sums_ref[unit // units, pl.ds(row, UNIT), :])
+        return jnp.concatenate(pieces, axis=0)
+
     lane = lax.broadcasted_iota(i32, (width, LANES), 1)
-    side = pltpu.roll(side, (n % 2) * HALF, 1)
-    tail = pltpu.roll(tail, (HALF - n * plan.tail) % LANES, 1)
-    out_ref[0, :, :LANES] = block(n)
-    out_ref[0, :, LANES:] = jnp.where(lane < HALF, side, tail)[:, : width - LANES]
-
-
-def unpacked(plan, total, own, count, units, base, lines):
-    width = plan.width
+
+    def square(ref, at, n, count, units, base):
+        side = pltpu.roll(block(count + n // 2, units, base), (n % 2) * HALF, 1)
+        tail = block(count + -(-count // 2), units, base)
+        tail = pltpu.roll(tail, (HALF + LANES - n * plan.tail) % LANES, 1)
+        ref[at, :, :LANES] = block(n, units, base)
+        ref[at, :, LANES:] = jnp.where(lane < HALF, side, tail)[:, : width - LANES]
+
+    def cross_step(k, carry):
+        p = turn * each[0] + k
+        base = (p // plan.own) * plan.cross_units * UNIT
+        square(cross_ref, k, p % plan.own, plan.own, plan.cross_units, base)
+        return carry
+
+    def diag_step(k, carry):
+        square(diag_ref, k, turn * each[1] + k, covs, plan.diag_units, plan.diag_at)
+        return carry
+
+    lax.fori_loop(0, each[0], cross_step, 0)
+    lax.fori_loop(0, each[1], diag_step, 0)
+
+    @pl.when(turn == 0)
+    def _():
+        at = covs * plan.tail
+        last = block(plan.diag_blocks - 1, plan.diag_units, plan.diag_at)
+        side_ref[...] = jnp.transpose(last)[at : at + covs]
+
+
+def unpacked(plan, core, mine, theirs):
+    width, pairs, covs = plan.width, plan.pairs, plan.covs
+    turns = math.gcd(pairs, covs)
+    each = (pairs // turns, covs // turns)
     return pl.pallas_call(
-        functools.partial(unpack_kernel, plan, own, count, units, base),
-        out_shape=jax.ShapeDtypeStruct((total, width, width), f32),
-        grid=(total,),
-        in_specs=[vmem()],
-        out_specs=pl.BlockSpec((1, width, width), lambda p: (p, 0, 0)),
+        functools.partial(unpack_kernel, plan, each),
+        out_shape=(
+            jax.ShapeDtypeStruct((pairs, width, width), f32),
+            jax.ShapeDtypeStruct((covs, width, width), f32),
+            jax.ShapeDtypeStruct((covs, width), f32),
+        ),
+        grid=(turns,),
+        in_specs=[smem(), vmem(), vmem()],
+        out_specs=(
+            pl.BlockSpec((each[0], width, width), lambda p: (p, 0, 0)),
+            pl.BlockSpec((each[1], width, width), lambda p: (p, 0, 0)),
+            pl.BlockSpec((covs, width), lambda p: (0, 0)),
+        ),
+        scratch_shapes=[pltpu.VMEM((plan.devices, plan.share, LANES), f32)],
         compiler_params=params(),
         name="unpacked",
-        cost_estimate=pl.CostEstimate(flops=10**6, bytes_accessed=14 * 10**6, transcendentals=0),
-    )(lines)
+        cost_estimate=pl.CostEstimate(flops=10**6, bytes_accessed=17 * 10**6, transcendentals=0),
+    )(core, mine, theirs)
 
 
 def clusters_of(groups):
@@ -432,44 +541,32 @@
     packets = picked_rows(plan, terms[:, 0], columns(pair_left), columns(pair_right % bins), basis)
     packets = lax.all_to_all(packets, "row", split_axis=0, concat_axis=0, tiled=True)
 
-    cov_w = sums[: plan.work_at].reshape(covs, bins)
-    work = sums[plan.work_at : plan.pair_at].reshape(covs, bins).astype(bf16)
-    work = jnp.pad(work, ((0, LANES - covs), (0, 0)))
-    rest = sums[plan.rest_at : plan.rest_at + -(-plan.padded // plan.rest_fold)]
-    pair_w = jnp.concatenate(
-        [
-            sums[plan.pair_at : plan.pair_at + plan.padded],
-            rest.reshape(-1, plan.rest)[: plan.padded],
-        ],
-        axis=1,
-    )
+    sums, packets = lax.optimization_barrier((sums, packets))
+    pair_w = sums[plan.pair_at : plan.pair_at + cluster * plan.member]
     if cluster > 1:
         pair_w = lax.all_to_all(
-            pair_w.reshape(cluster, plan.own, pair_block), "grp", 0, 0,
+            pair_w.reshape(cluster, plan.member, LANES), "grp", 0, 0,
             axis_index_groups=clusters, tiled=True,
-        ).reshape(plan.padded, pair_block)
-
-    mine, theirs = products(plan, core, terms[:, 1], packets, pair_w, cov_w, work, basis)
+        ).reshape(cluster * plan.member, LANES)
+
+    mine, theirs = products(plan, core, terms[:, 1], packets, pair_w, sums, basis)
     total = mine + lax.ppermute(theirs, "row", swap)
     total = lax.psum_scatter(total, "row", axis_index_groups=rings, tiled=True)
-    total = lax.optimization_barrier(total).astype(bf16)
-    cross = total[: plan.diag_at]
+    chunks = packed(plan, total)
     if cluster > 1:
         cross = lax.all_to_all(
-            cross.reshape(cluster, -1, LANES), "grp", 0, 0, axis_index_groups=clusters, tiled=True
-        ).reshape(plan.diag_at, LANES)
-    share = jnp.concatenate([cross, total[plan.diag_at :]], axis=0)
-    lines = lax.all_gather(share, "row", axis=0, tiled=True).reshape(devices, plan.share, LANES)
-
-    cross_blocks = unpacked(plan, pairs, plan.own, plan.own, plan.cross_units, 0, lines)
-    diag_blocks = unpacked(plan, covs, covs, covs, plan.diag_units, plan.diag_at, lines)
-    side = []
-    for cut in range(plan.cuts):
-        unit = (plan.diag_blocks - 1) * plan.cuts + cut
-        row = plan.diag_at + (unit % plan.diag_units) * UNIT
-        side.append(lines[unit // plan.diag_units, row : row + UNIT])
-    at = covs * plan.tail
-    basis_response = jnp.transpose(jnp.concatenate(side, axis=0)[:, at : at + covs]).astype(f32)
+            chunks[:cluster], "grp", 0, 0, axis_index_groups=clusters, tiled=True
+        )
+        chunks = jnp.concatenate([cross, chunks[cluster:]], axis=0)
+    length = chunks.shape[0] * plan.chunk
+    mine = lax.all_gather(
+        chunks.reshape(length, LANES), "row", axis=0, axis_index_groups=rings, tiled=True
+    )
+    theirs = lax.ppermute(mine, "row", swap)
+    shape = (plan.chips, length, LANES)
+    cross_blocks, diag_blocks, basis_response = unpacked(
+        plan, core, mine.reshape(shape), theirs.reshape(shape)
+    )
     return diag_blocks, cross_blocks, basis_response
 
 

time: 426 us -> 345 us (0.81)
  waiting for transfers between devices: 254 us -> 90.6 us
  blocking collectives: 0 us -> 112 us
  Pallas kernels: 95.7 us -> 73.8 us
  local copies, waits for them, and re-layouts: 13.8 us -> 7.57 us
    all_gather x1 -> x0, waiting for transfers between devices: 79.5 us -> none  [on_device(): lax.all_gather(share, 'row', axis=0, tiled=True)]
    all_to_all x0 -> x2, blocking collectives: none -> 72 us  [the longest x1 64.3 us: on_device(): lax.all_to_all(packets, 'row', split_axis=0, concat_axis=0, tiled=True)]
    reduce_scatter x1, waiting for transfers between devices: 53.8 us -> 5.01 us  [on_device(): sums = lax.psum_scatter(sums, 'row', axis_index_groups=rings, tiled=True)]
    all_to_all x3 -> x1, waiting for transfers between devices: 47.4 us -> 3.11 us  [on_device(): lax.all_to_all(chunks[:cluster], 'grp', 0, 0, axis_index_groups=clusters,...]
    all_gather x0 -> x1, blocking collectives: none -> 40 us  [on_device(): lax.all_gather(chunks.reshape(length, LANES), 'row', axis=0, axis_index_g...]
    all_to_all x3 -> x1, starting transfers between devices: 27.1 us -> 3.71 us  [on_device(): lax.all_to_all(chunks[:cluster], 'grp', 0, 0, axis_index_groups=clusters,...]
    ppermute x0 -> x1, starting transfers between devices: none -> 16.6 us  [on_device(): theirs = lax.ppermute(mine, 'row', swap)]
    pallas_call x2, Pallas kernels: 28.5 us -> 17.1 us  [the longest x1 15.3 us: unpacked(): pl.pallas_call(functools.partial(unpack_kernel, plan, each), out_shape=(j...]
  transfers between devices with their start and end apart: 8 -> 6, of which waited for: 7 -> 6; matrix products, arithmetic and copies ran while one was open for 2% -> 1% of each run, Pallas kernels for 2% -> 3%
where the time goes in v2:
time: 345 us; the launch traced here: 344 us
  blocking collectives  112 us (32%)
  waiting for transfers between devices  90.6 us (26%)
  Pallas kernels  73.8 us (21%)
  starting transfers between devices  39 us (11%)
  between operations  14.2 us (4%)
  local copies, waits for them, and re-layouts  7.57 us (2%)
  other arithmetic  7.25 us (2%)
    unnamed x3, waiting for transfers between devices  66.4 us
    all_to_all x1, blocking collectives, on_device(): lax.all_to_all(packets, 'row', split_axis=0, concat_axis=0, tiled=True)  64.3 us
    all_gather x1, blocking collectives, on_device(): lax.all_gather(chunks.reshape(length, LANES), 'row', axis=0, axis_index_g...  40 us
    pallas_call x1, Pallas kernels, products(): pl.pallas_call(functools.partial(product_kernel, plan), out_shape=(out, o...  25.4 us
    pallas_call x1, Pallas kernels, histograms(): pl.pallas_call(functools.partial(hist_kernel, plan), out_shape=(out, out)...  22.3 us
    ppermute x1, starting transfers between devices, on_device(): theirs = lax.ppermute(mine, 'row', swap)  16.6 us
    pallas_call x1, Pallas kernels, unpacked(): pl.pallas_call(functools.partial(unpack_kernel, plan, each), out_shape=(j...  15.3 us
    ppermute x1, starting transfers between devices, on_device(): sums = mine + lax.ppermute(theirs, 'row', swap)  9.9 us
  transfers between devices with their start and end apart: 6, of which 6 were waited for; matrix products, arithmetic and copies ran while one was open for 1% of the time, Pallas kernels for 3%

profile of v2, /device:TPU:69, one launch (start us, length us, event | category | flops | bytes accessed | tf_op | source)
XLA Modules:
  0.0 344.4 jit_solution(1741621891021234905)
XLA Ops:
  7.2 0.1 reduce-scatter.5.cloned.1.call-start
  7.3 0.0 copy-start.2
  7.3 0.0 copy-start.3
  7.3 22.3 %histograms.1 = (f32[3584,128]{1,0:T(8,128)}, f32[3584,128]{1,0:T(8,128)}) custom-call(s32[1]{0:T(128)} %bitcast.core_ref, s32[10,2048]{1,0:T(8,128)} %bitcast.32, s32[45,2048]{1,0:T(8,128)} %bitcast.31, f32[1,2048]{1,0:T(1,128)} %bitcast.33, f32[1,2048]{1,0:T(1,128)} %bitcast.34), custom_call_target="tpu_custom_call" | custom-call | flops 12000000000 | bytes 8000000 | tf_op jit(solution)/shard_map/histograms/pallas_call | solution.py:165
  29.6 9.9 %collective-permute-start = (f32[3584,128]{1,0:T(8,128)}, f32[3584,128]{1,0:T(8,128)S(1)}, u32[]{:S(2)}, u32[]{:S(2)}) collective-permute-start(f32[3584,128]{1,0:T(8,128)} %get-tuple-element.13), channel_id=1, source_target_pairs={{0,1},{1,0},{2,3},{3,2},{4,5},{5,4},{6,7},{7,6},{8,9},{9,8},{10,11... | collective-permute-start | bytes 5505032 | tf_op jit(solution)/shard_map/ppermute | solution.py:529
  39.5 0.0 copy-done.2
  39.5 0.0 copy-done.3
  39.5 3.6 %collective-permute-done = f32[3584,128]{1,0:T(8,128)S(1)} collective-permute-done((f32[3584,128]{1,0:T(8,128)}, f32[3584,128]{1,0:T(8,128)S(1)}, u32[]{:S(2)}, u32[]{:S(2)}) %collective-permute-start) | collective-permute-done | bytes 1835040 | tf_op jit(solution)/shard_map/ppermute | solution.py:529
  43.1 0.0 copy-start.4
  43.1 2.9 add.37
  46.0 0.1 reduce-scatter.5.cloned.1.call-update
  46.1 0.1 reduce-scatter.7.cloned.1.call-start
  46.1 0.0 copy-done.4
  46.1 0.1 pad_dynamic-slice_fusion.2
  46.2 0.2 reshape.49
  46.4 1.0 copy.15
  47.4 0.2 reshape.47
  47.6 1.0 copy.14
  48.6 0.5 slice_bitcast_fusion
  49.1 9.0 %picked_rows.1 = bf16[32,104,128]{2,1,0:T(8,128)(2,1)} custom-call(s32[12]{0:T(128)} %get-tuple-element.21.terms_ref, s32[160,12]{1,0:T(8,128)} %bitcast.28, s32[160,12]{1,0:T(8,128)} %bitcast.27, bf16[10,200,1024]{2,1,0:T(8,128)(2,1)} %bitcast.21), custom_call_target="tpu_custom_call" | custom-call | flops 1000000000 | bytes 6000000 | tf_op jit(solution)/shard_map/picked_rows/pallas_call | solution.py:227
  58.1 64.3 %all_to_all.15.packet_ref = bf16[32,104,128]{2,1,0:T(8,128)(2,1)} all-to-all(bf16[32,104,128]{2,1,0:T(8,128)(2,1)} %picked_rows.1), channel_id=1, replica_groups=mesh['grp'=4,'row'=32] {'row'}, dimensions={0} | all-to-all | bytes 1703936 | tf_op jit(solution)/shard_map/all_to_all | solution.py:542
  122.5 5.0 %reduce-scatter.5.cloned.1.call-done.weights_ref = f32[224,128]{1,0:T(8,128)} async-done(((f32[3584,128]{1,0:T(8,128)}), f32[224,128]{1,0:T(8,128)}) %reduce-scatter.5.cloned.1.call-update) | async-done | bytes 114704 | tf_op jit(solution)/shard_map/reduce_scatter | solution.py:530
  127.5 0.8 slice.17
  128.2 7.7 %all_to_all.16 = f32[4,16,128]{2,1,0:T(8,128)} all-to-all(f32[4,16,128]{2,1,0:T(8,128)S(1)} %bitcast.29), channel_id=1, replica_groups={{0,32,64,96},{1,33,65,97},{2,34,66,98},{3,35,67,99},{4,36,68,100},{5,37..., dimensions={0} | all-to-all | bytes 65536 | tf_op jit(solution)/shard_map/all_to_all | solution.py:547
  135.9 25.4 %products.1 = (f32[9600,128]{1,0:T(8,128)}, f32[9600,128]{1,0:T(8,128)}) custom-call(s32[1]{0:T(128)} %bitcast.core_ref, s32[12]{0:T(128)} %get-tuple-element.22.terms_ref, bf16[32,104,128]{2,1,0:T(8,128)(2,1)} %all_to_all.15.packet_ref, f32[64,128]{1,0:T(8,128)} %bitcast.30, f32[224,128]{1,0:T(8,128)} %reduce-scatter.5.cloned.1.call-done.weights_ref, ...), custom_call_target="tpu_custom_call" | custom-call | flops 4000000000 | bytes 26000000 | tf_op jit(solution)/shard_map/products/pallas_call | solution.py:366
  161.3 8.7 %collective-permute-start.1 = (f32[9600,128]{1,0:T(8,128)}, f32[9600,128]{1,0:T(8,128)S(1)}, u32[]{:S(2)}, u32[]{:S(2)}) collective-permute-start(f32[9600,128]{1,0:T(8,128)} %get-tuple-element.17), channel_id=1, source_target_pairs={{0,1},{1,0},{2,3},{3,2},{4,5},{5,4},{6,7},{7,6},{8,9},{9,8},{10,11... | collective-permute-start | bytes 14745608 | tf_op jit(solution)/shard_map/ppermute | solution.py:553
  170.1 8.0 %collective-permute-done.1 = f32[9600,128]{1,0:T(8,128)S(1)} collective-permute-done((f32[9600,128]{1,0:T(8,128)}, f32[9600,128]{1,0:T(8,128)S(1)}, u32[]{:S(2)}, u32[]{:S(2)}) %collective-permute-start.1) | collective-permute-done | bytes 4915232 | tf_op jit(solution)/shard_map/ppermute | solution.py:553
  178.1 4.3 %add.39 = f32[9600,128]{1,0:T(8,128)} add(f32[9600,128]{1,0:T(8,128)} %get-tuple-element.16, f32[9600,128]{1,0:T(8,128)S(1)} %collective-permute-done.1) | non-fusion elementwise | flops 1228800 | bytes 14745600 | tf_op jit(solution)/shard_map/add | solution.py:553
  182.4 0.1 reduce-scatter.7.cloned.1.call-update
  182.5 66.3 %reduce-scatter.7.cloned.1.call-done.in_ref = f32[600,128]{1,0:T(8,128)} async-done(((f32[9600,128]{1,0:T(8,128)}), f32[600,128]{1,0:T(8,128)}) %reduce-scatter.7.cloned.1.call-update) | async-done | bytes 307216
  248.7 1.8 packed.1
  250.5 1.6 slice.20
  252.1 3.7 %all-to-all-start.2 = ((s16[4,128,128]{2,1,0:T(8,128)(2,1)}), s16[4,128,128]{2,1,0:T(8,128)(2,1)S(1)}, u32[]{:S(2)}, u32[]{:S(2)}) async-start(s16[4,128,128]{2,1,0:T(8,128)(2,1)} %slice.20), calls=%async_computation.3 | async-start | bytes 262144 | tf_op jit(solution)/shard_map/all_to_all | solution.py:557
  255.8 0.8 slice.21
  256.6 3.1 all-to-all-done.2
  259.7 40.0 %all-gather.1 = s16[10240,128]{1,0:T(8,128)(2,1)S(1)} all-gather(s16[640,128]{1,0:T(8,128)(2,1)S(1)} %bitcast.26), channel_id=1, replica_groups={{0,2,4,6,8,10,12,14,16,18,20,22,24,26,28,30},{1,3,5,7,9,11,13,15,17,19,..., dimensions={0}, use_global_device_ids=true | all-gather | bytes 2785280 | tf_op jit(solution)/shard_map/all_gather | solution.py:562
  299.7 0.0 copy-start
  299.7 16.6 %collective-permute-start.2 = (s16[10240,128]{1,0:T(8,128)(2,1)S(1)}, s16[10240,128]{1,0:T(8,128)(2,1)S(1)}, u32[]{:S(2)}, u32[]{:S(2)}) collective-permute-start(s16[10240,128]{1,0:T(8,128)(2,1)S(1)} %all-gather.1), channel_id=1, source_target_pairs={{0,1},{1,0},{2,3},{3,2},{4,5},{5,4},{6,7},{7,6},{8,9},{9,8},{10,11... | collective-permute-start | bytes 7864328 | tf_op jit(solution)/shard_map/ppermute | solution.py:565
  316.2 4.5 %collective-permute-done.2 = s16[10240,128]{1,0:T(8,128)(2,1)S(1)} collective-permute-done((s16[10240,128]{1,0:T(8,128)(2,1)S(1)}, s16[10240,128]{1,0:T(8,128)(2,1)S(1)}, u32[]{:S(2)}, u32[]{:S(2)}) %collective-permute-start.2) | collective-permute-done | bytes 2621472 | tf_op jit(solution)/shard_map/ppermute | solution.py:565
  320.8 0.0 copy-start.1
  320.8 1.5 copy-done.1
  322.3 0.0 copy-done
  322.3 15.3 %unpacked.1 = (f32[45,200,200]{2,1,0:T(8,128)}, f32[10,200,200]{2,1,0:T(8,128)}, f32[10,200]{1,0:T(8,128)}) custom-call(s32[1]{0:T(128)} %bitcast.core_ref, s16[16,640,128]{2,1,0:T(8,128)(2,1)} %bitcast.20, s16[16,640,128]{2,1,0:T(8,128)(2,1)} %bitcast.23), custom_call_target="tpu_custom_call" | custom-call | flops 1000000 | bytes 17000000 | tf_op jit(solution)/shard_map/unpacked/pallas_call | solution.py:469
  (3 shorter events, 0.1 us)
Async XLA Ops:
  7.2 120.3 %reduce-scatter.5.cloned.1.call-start = ((), (), s32[]{:S(2)}) async-start(), calls=%async_computation.5 | async-start | bytes 1949696 | tf_op jit(solution)/shard_map/reduce_scatter | solution.py:530
  7.3 32.2 %copy-start.2 = (s32[45,160]{1,0:T(8,128)S(1)}, s32[45,160]{1,0:T(8,128)}, u32[]{:S(2)}) copy-start(s32[45,160]{1,0:T(8,128)} %param.15) | copy-start | bytes 86404
  7.3 32.2 %copy-start.3 = (s32[45,160]{1,0:T(8,128)S(1)}, s32[45,160]{1,0:T(8,128)}, u32[]{:S(2)}) copy-start(s32[45,160]{1,0:T(8,128)} %param.14) | copy-start | bytes 86404
  29.6 13.5 %collective-permute-start = (f32[3584,128]{1,0:T(8,128)}, f32[3584,128]{1,0:T(8,128)S(1)}, u32[]{:S(2)}, u32[]{:S(2)}) collective-permute-start(f32[3584,128]{1,0:T(8,128)} %get-tuple-element.13), channel_id=1, source_target_pairs={{0,1},{1,0},{2,3},{3,2},{4,5},{5,4},{6,7},{7,6},{8,9},{9,8},{10,11... | collective-permute-start | bytes 5505032 | tf_op jit(solution)/shard_map/ppermute | solution.py:529
  43.1 3.1 copy-start.4
  46.1 202.7 %reduce-scatter.7.cloned.1.call-start = ((), (), s32[]{:S(2)}) async-start(), calls=%async_computation.6 | async-start | bytes 5222400
  161.3 16.8 %collective-permute-start.1 = (f32[9600,128]{1,0:T(8,128)}, f32[9600,128]{1,0:T(8,128)S(1)}, u32[]{:S(2)}, u32[]{:S(2)}) collective-permute-start(f32[9600,128]{1,0:T(8,128)} %get-tuple-element.17), channel_id=1, source_target_pairs={{0,1},{1,0},{2,3},{3,2},{4,5},{5,4},{6,7},{7,6},{8,9},{9,8},{10,11... | collective-permute-start | bytes 14745608 | tf_op jit(solution)/shard_map/ppermute | solution.py:553
  252.1 7.6 %all-to-all-start.2 = ((s16[4,128,128]{2,1,0:T(8,128)(2,1)}), s16[4,128,128]{2,1,0:T(8,128)(2,1)S(1)}, u32[]{:S(2)}, u32[]{:S(2)}) async-start(s16[4,128,128]{2,1,0:T(8,128)(2,1)} %slice.20), calls=%async_computation.3 | async-start | bytes 262144 | tf_op jit(solution)/shard_map/all_to_all | solution.py:557
  299.7 22.6 %copy-start = (s16[10240,128]{1,0:T(8,128)(2,1)}, s16[10240,128]{1,0:T(8,128)(2,1)S(1)}, u32[]{:S(2)}) copy-start(s16[10240,128]{1,0:T(8,128)(2,1)S(1)} %all-gather.1) | copy-start | bytes 7864324
  299.7 21.1 %collective-permute-start.2 = (s16[10240,128]{1,0:T(8,128)(2,1)S(1)}, s16[10240,128]{1,0:T(8,128)(2,1)S(1)}, u32[]{:S(2)}, u32[]{:S(2)}) collective-permute-start(s16[10240,128]{1,0:T(8,128)(2,1)S(1)} %all-gather.1), channel_id=1, source_target_pairs={{0,1},{1,0},{2,3},{3,2},{4,5},{5,4},{6,7},{7,6},{8,9},{9,8},{10,11... | collective-permute-start | bytes 7864328 | tf_op jit(solution)/shard_map/ppermute | solution.py:565
  320.8 1.5 copy-start.1
Sparse Core Ops, SparseCore 0:
  46.2 81.2 reduce-scatter.4
  182.6 66.1 reduce-scatter.6

commit v3 on v2

--- a/solution.py
+++ b/solution.py
@@ -236,13 +236,70 @@
     )(terms, left, right, basis)
 
 
-def product_kernel(
-    plan, core_ref, terms_ref, packet_ref, pair_w_ref, weights_ref, basis_ref,
-    mine_ref, theirs_ref, a_ref, b_ref, work_ref, sums_ref,
-):
-    core = core_ref[0]
-    devices, slot, chips = plan.devices, plan.slot, plan.chips
-    width, own = plan.width, plan.own
+class Blocks:
+    def __init__(self, plan, core, sums_ref, share):
+        self.plan, self.core, self.sums, self.share = plan, core, sums_ref, share
+
+    def spot(self, block, cut, units, base):
+        unit = block * self.plan.cuts + cut
+        owner = unit // units
+        place = ((owner & 1) ^ self.core) * self.plan.chips + lax.shift_right_logical(owner, 1)
+        return pl.multiple_of(place * self.share + base + (unit % units) * UNIT, 8)
+
+    def put(self, block, value, units, base, first=None, last=None):
+        for cut in range(self.plan.cuts):
+            where = pl.ds(self.spot(block, cut, units, base), UNIT)
+            piece = value[cut * UNIT : (cut + 1) * UNIT]
+            if first is not None:
+                lane = lax.broadcasted_iota(i32, (UNIT, LANES), 1)
+                keep = (lane >= first) & (lane < last)
+                piece = jnp.where(keep, piece, self.sums[where, :])
+            self.sums[where, :] = piece
+
+    def put_square(self, n, count, square, units, base):
+        width, tail = self.plan.width, self.plan.tail
+        self.put(n, square[:, :LANES], units, base)
+        rest = width - LANES
+        side = jnp.concatenate([square[:, LANES:], jnp.zeros((width, LANES - rest), f32)], axis=1)
+        at = (n % 2) * HALF
+        self.put(count + n // 2, pltpu.roll(side, at, 1), units, base, at, at + HALF)
+        at = n * tail
+        moved = pltpu.roll(side, (at + HALF) % LANES, 1)
+        self.put(count + -(-count // 2), moved, units, base, at, at + tail)
+
+    def clear(self, count, units, base):
+        plan = self.plan
+        blocks = plan.blocks_of(count)
+        parts = [(blocks - 1) * plan.cuts + c for c in range(plan.cuts)]
+        parts += list(range(blocks * plan.cuts, units * plan.devices))
+        if count % 2:
+            parts += [(blocks - 2) * plan.cuts + c for c in range(plan.cuts)]
+        for unit in parts:
+            where = pl.ds(self.spot(unit // plan.cuts, unit % plan.cuts, units, base), UNIT)
+            self.sums[where, :] = jnp.zeros((UNIT, LANES), f32)
+
+    def finish(self, mine_ref, theirs_ref):
+        half = self.plan.chips * self.share
+        mine_ref[...] = self.sums[:half, :]
+        theirs_ref[...] = self.sums[half:, :]
+
+
+def sums_call(plan, kernel, name, share, flops, scratch, ins, *args):
+    out = jax.ShapeDtypeStruct((plan.chips * share, LANES), f32)
+    return pl.pallas_call(
+        kernel,
+        out_shape=(out, out),
+        in_specs=ins,
+        out_specs=(vmem(), vmem()),
+        scratch_shapes=scratch + [pltpu.VMEM((2 * plan.chips * share, LANES), f32)],
+        compiler_params=params(),
+        name=name,
+        cost_estimate=pl.CostEstimate(flops=flops, bytes_accessed=6 * 10**6, transcendentals=0),
+    )(*args)
+
+
+def ready_kernel(plan, terms_ref, packet_ref, basis_ref, left_ref, right_ref, a_ref, b_ref):
+    devices, slot, own = plan.devices, plan.slot, plan.own
     half = slot // 2
 
     def unpack(o, carry):
@@ -264,51 +321,44 @@
         return carry
 
     lax.fori_loop(0, devices, unpack, 0)
-
-    def spot(block, cut, units, base):
-        unit = block * plan.cuts + cut
-        owner = unit // units
-        place = ((owner & 1) ^ core) * chips + lax.shift_right_logical(owner, 1)
-        return pl.multiple_of(place * plan.share + base + (unit % units) * UNIT, 8)
-
-    def put(block, value, units, base, first=None, last=None):
-        for cut in range(plan.cuts):
-            where = pl.ds(spot(block, cut, units, base), UNIT)
-            piece = value[cut * UNIT : (cut + 1) * UNIT]
-            if first is None:
-                sums_ref[where, :] = piece
-            else:
-                lane = lax.broadcasted_iota(i32, (UNIT, LANES), 1)
-                keep = (lane >= first) & (lane < last)
-                sums_ref[where, :] = jnp.where(keep, piece, sums_ref[where, :])
-
-    def put_square(n, count, square, units, base):
-        put(n, square[:, :LANES], units, base)
-        rest = width - LANES
-        side = jnp.concatenate([square[:, LANES:], jnp.zeros((width, LANES - rest), f32)], axis=1)
-        at = (n % 2) * HALF
-        put(count + n // 2, pltpu.roll(side, at, 1), units, base, at, at + HALF)
-        tail_at = n * plan.tail
-        put(
-            count + -(-count // 2),
-            pltpu.roll(side, (tail_at + HALF) % LANES, 1),
-            units, base, tail_at, tail_at + plan.tail,
-        )
-
-    def clear(count, units, base):
-        blocks = plan.blocks_of(count)
-        parts = [(blocks - 1) * plan.cuts + c for c in range(plan.cuts)]
-        parts += list(range(blocks * plan.cuts, units * devices))
-        if count % 2:
-            parts += [(blocks - 2) * plan.cuts + c for c in range(plan.cuts)]
-        for unit in parts:
-            where = pl.ds(spot(unit // plan.cuts, unit % plan.cuts, units, base), UNIT)
-            sums_ref[where, :] = jnp.zeros((UNIT, LANES), f32)
-
-    for m in range(plan.cluster):
-        clear(own, plan.cross_units, m * plan.cross_units * UNIT)
-    clear(plan.covs, plan.diag_units, plan.diag_at)
-
+    across = lax.broadcasted_iota(i32, (plan.pair_block, plan.bins), 1)
+    extra = plan.width - LANES
+
+    def pair_step(i, carry):
+        stride = [pl.ds(j * own + i, devices, stride=slot) for j in range(plan.per)]
+        a = jnp.concatenate([a_ref[s, :] for s in stride], axis=0)
+        b = jnp.concatenate([b_ref[s, :] for s in stride], axis=0)
+        index = (b[:, extra : extra + 1] * 32.0 + b[:, extra + 1 : extra + 2]).astype(i32)
+        hot = (across == index).astype(f32).astype(bf16)
+        right_ref[i] = dot(hot, basis_ref[terms_ref[i]], NT).astype(bf16)
+        left = jnp.concatenate([jnp.transpose(a), jnp.transpose(b)[:extra]], axis=0)
+        left_ref[i] = left.astype(bf16)
+        return carry
+
+    lax.fori_loop(0, own, pair_step, 0)
+
+
+def ready_rows(plan, terms, packets, basis):
+    own, width, block = plan.own, plan.width, plan.pair_block
+    return pl.pallas_call(
+        functools.partial(ready_kernel, plan),
+        out_shape=(
+            jax.ShapeDtypeStruct((own, width, block), bf16),
+            jax.ShapeDtypeStruct((own, block, width), bf16),
+        ),
+        in_specs=[smem(), vmem(), vmem()],
+        out_specs=(vmem(), vmem()),
+        scratch_shapes=[pltpu.VMEM((plan.devices * plan.slot, LANES), f32)] * 2,
+        compiler_params=params(),
+        name="ready_rows",
+        cost_estimate=pl.CostEstimate(flops=10**9, bytes_accessed=7 * 10**6, transcendentals=0),
+    )(terms, packets, basis)
+
+
+def diag_kernel(plan, core_ref, weights_ref, basis_ref, mine_ref, theirs_ref, work_ref, sums_ref):
+    width, units = plan.width, plan.diag_units
+    blocks = Blocks(plan, core_ref[0], sums_ref, units * UNIT)
+    blocks.clear(plan.covs, units, 0)
     lines = plan.bins // LANES
     work_ref[...] = jnp.zeros_like(work_ref)
     for j in range(plan.covs):
@@ -323,60 +373,76 @@
         rows = weights_ref[pl.ds(pl.multiple_of(j * lines, lines), lines), :]
         weight = jnp.concatenate([rows[t : t + 1] for t in range(lines)], axis=1)
         weighted = (basis.astype(f32) * weight).astype(bf16)
-        square = dot(weighted, basis, NT)
-        put_square(j, plan.covs, square, plan.diag_units, plan.diag_at)
+        blocks.put_square(j, plan.covs, dot(weighted, basis, NT), units, 0)
         return jnp.where(column == j, dot(basis, work, NT), side)
 
     side = lax.fori_loop(0, plan.covs, diag_step, jnp.zeros(column.shape, f32))
     at = plan.covs * plan.tail
     side = jnp.concatenate([side, jnp.zeros((width, LANES - side.shape[1]), f32)], axis=1)
-    put(
-        plan.diag_blocks - 1, pltpu.roll(side, at, 1),
-        plan.diag_units, plan.diag_at, at, at + plan.covs,
+    blocks.put(plan.diag_blocks - 1, pltpu.roll(side, at, 1), units, 0, at, at + plan.covs)
+    blocks.finish(mine_ref, theirs_ref)
+
+
+def diag_sums(plan, core, weights, basis):
+    work = pltpu.VMEM((up(plan.covs, 16), plan.bins), f32)
+    return sums_call(
+        plan, functools.partial(diag_kernel, plan), "diag_sums", plan.diag_units * UNIT, 10**9,
+        [work], [smem(), vmem(), vmem()], core, weights, basis,
     )
 
-    across = lax.broadcasted_iota(i32, (plan.pair_block, plan.bins), 1)
-    extra = width - LANES
+
+def cross_kernel(plan, first, count, core_ref, pair_w_ref, left_ref, right_ref, mine_ref, theirs_ref, sums_ref):
+    own, units = plan.own, plan.cross_units
+    blocks = Blocks(plan, core_ref[0], sums_ref, count * units * UNIT)
+    for m in range(count):
+        blocks.clear(own, units, m * units * UNIT)
 
     def pair_step(i, carry):
-        stride = [pl.ds(j * own + i, devices, stride=slot) for j in range(plan.per)]
-        a = jnp.concatenate([a_ref[s, :] for s in stride], axis=0)
-        b = jnp.concatenate([b_ref[s, :] for s in stride], axis=0)
-        index = (b[:, extra : extra + 1] * 32.0 + b[:, extra + 1 : extra + 2]).astype(i32)
-        hot = (across == index).astype(f32).astype(bf16)
-        right = dot(hot, basis_ref[terms_ref[i]], NT).astype(bf16)
-        left = jnp.concatenate([jnp.transpose(a), jnp.transpose(b)[:extra]], axis=0)
-        for m in range(plan.cluster):
-            start = m * plan.member
+        left, right = left_ref[i].astype(f32), right_ref[i]
+        for m in range(count):
+            start = (first + m) * plan.member
             turn = (LANES - (i % plan.rest_fold) * plan.rest) % LANES
             rest = pair_w_ref[pl.ds(start + own + i // plan.rest_fold, 1), :]
             rest = pltpu.roll(jnp.broadcast_to(rest, (8, LANES)), turn, 1)[:1, : plan.rest]
             weight = jnp.concatenate([pair_w_ref[pl.ds(start + i, 1), :], rest], axis=1)
             square = dot((left * weight).astype(bf16), right, NN)
-            put_square(i, own, square, plan.cross_units, m * plan.cross_units * UNIT)
+            blocks.put_square(i, own, square, units, m * units * UNIT)
         return carry
 
     lax.fori_loop(0, own, pair_step, 0)
-    mine_ref[...] = sums_ref[: chips * plan.share, :]
-    theirs_ref[...] = sums_ref[chips * plan.share :, :]
-
-
-def products(plan, core, terms, packets, pair_w, weights, basis):
-    out = jax.ShapeDtypeStruct((plan.chips * plan.share, LANES), f32)
+    blocks.finish(mine_ref, theirs_ref)
+
+
+def cross_sums(plan, first, count, core, pair_w, left, right):
+    return sums_call(
+        plan, functools.partial(cross_kernel, plan, first, count), "cross_sums",
+        count * plan.cross_units * UNIT, 10**9, [], [smem(), vmem(), vmem(), vmem()],
+        core, pair_w, left, right,
+    )
+
+
+def add_kernel(*refs):
+    out_ref = refs[-1]
+    at = 0
+    for mine_ref, got_ref in zip(refs[:-1:2], refs[1:-1:2]):
+        rows = mine_ref.shape[0]
+        out_ref[at : at + rows, :] = mine_ref[...] + got_ref[...]
+        at += rows
+
+
+def added(plan, parts):
+    flat = [array for pair in parts for array in pair]
+    rows = [array.shape[0] // plan.chips for array in flat]
     return pl.pallas_call(
-        functools.partial(product_kernel, plan),
-        out_shape=(out, out),
-        in_specs=[smem(), smem()] + [vmem()] * 4,
-        out_specs=(vmem(), vmem()),
-        scratch_shapes=[pltpu.VMEM((plan.devices * plan.slot, LANES), f32)] * 2
-        + [
-            pltpu.VMEM((up(plan.covs, 16), plan.bins), f32),
-            pltpu.VMEM((2 * plan.chips * plan.share, LANES), f32),
-        ],
+        add_kernel,
+        out_shape=jax.ShapeDtypeStruct((plan.chips * plan.share, LANES), f32),
+        grid=(plan.chips,),
+        in_specs=[pl.BlockSpec((r, LANES), lambda z: (z, 0)) for r in rows],
+        out_specs=pl.BlockSpec((plan.share, LANES), lambda z: (z, 0)),
         compiler_params=params(),
-        name="products",
-        cost_estimate=pl.CostEstimate(flops=4 * 10**9, bytes_accessed=26 * 10**6, transcendentals=0),
-    )(core, terms, packets, pair_w, weights, basis)
+        name="added",
+        cost_estimate=pl.CostEstimate(flops=10**6, bytes_accessed=15 * 10**6, transcendentals=0),
+    )(*flat)
 
 
 def pack_kernel(plan, in_ref, out_ref):
@@ -541,16 +607,21 @@
     packets = picked_rows(plan, terms[:, 0], columns(pair_left), columns(pair_right % bins), basis)
     packets = lax.all_to_all(packets, "row", split_axis=0, concat_axis=0, tiled=True)
 
-    sums, packets = lax.optimization_barrier((sums, packets))
+    left, right = ready_rows(plan, terms[:, 1], packets, basis)
+    sums, left, right = lax.optimization_barrier((sums, left, right))
     pair_w = sums[plan.pair_at : plan.pair_at + cluster * plan.member]
     if cluster > 1:
         pair_w = lax.all_to_all(
             pair_w.reshape(cluster, plan.member, LANES), "grp", 0, 0,
             axis_index_groups=clusters, tiled=True,
         ).reshape(cluster * plan.member, LANES)
-
-    mine, theirs = products(plan, core, terms[:, 1], packets, pair_w, sums, basis)
-    total = mine + lax.ppermute(theirs, "row", swap)
+    diag = diag_sums(plan, core, sums, basis)
+    step = -(-cluster // 2)
+    parts = [
+        cross_sums(plan, first, min(step, cluster - first), core, pair_w, left, right)
+        for first in range(0, cluster, step)
+    ] + [diag]
+    total = added(plan, [(mine, lax.ppermute(theirs, "row", swap)) for mine, theirs in parts])
     total = lax.psum_scatter(total, "row", axis_index_groups=rings, tiled=True)
     chunks = packed(plan, total)
     if cluster > 1:

time: 345 us -> 350 us (1.014)
  Pallas kernels: 73.8 us -> 96.4 us
  waiting for transfers between devices: 90.6 us -> 78.6 us
  other arithmetic: 7.25 us -> 2.94 us
    pallas_call x1 -> x5, Pallas kernels: 25.4 us -> 48 us  [the longest x3 25.4 us: sums_call(): pl.pallas_call(kernel, out_shape=(out, out), in_specs=ins, out_specs=(vme...]
    ppermute x1 -> x3, waiting for transfers between devices: 8.03 us -> 2.41 us  [on_device(): lax.ppermute(theirs, 'row', swap)]
    reduce_scatter x1, waiting for transfers between devices: 5.01 us -> 0.01 us  [on_device(): sums = lax.psum_scatter(sums, 'row', axis_index_groups=rings, tiled=True)]
    add x1 -> x0, other arithmetic: 4.29 us -> none  [on_device(): total = mine + lax.ppermute(theirs, 'row', swap)]
    ppermute x1 -> x3, starting transfers between devices: 8.75 us -> 5.14 us  [on_device(): lax.ppermute(theirs, 'row', swap)]
  transfers between devices with their start and end apart: 6 -> 8, of which waited for: 6 -> 5; matrix products, arithmetic and copies ran while one was open for 1% -> 1% of each run, Pallas kernels for 3% -> 8%
where the time goes in v3:
time: 350 us; the launch traced here: 348 us
  blocking collectives  110 us (31%)
  Pallas kernels  96.4 us (28%)
  waiting for transfers between devices  78.6 us (22%)
  starting transfers between devices  36 us (10%)
  between operations  14.2 us (4%)
  local copies, waits for them, and re-layouts  9.8 us (3%)
    unnamed x3, waiting for transfers between devices  67.5 us
    all_to_all x1, blocking collectives, on_device(): lax.all_to_all(packets, 'row', split_axis=0, concat_axis=0, tiled=True)  64.5 us
    all_gather x1, blocking collectives, on_device(): lax.all_gather(chunks.reshape(length, LANES), 'row', axis=0, axis_index_g...  39 us
    pallas_call x3, Pallas kernels, sums_call(): pl.pallas_call(kernel, out_shape=(out, out), in_specs=ins, out_specs=(vme...  25.4 us
    pallas_call x1, Pallas kernels, histograms(): pl.pallas_call(functools.partial(hist_kernel, plan), out_shape=(out, out)...  22.3 us
    ppermute x1, starting transfers between devices, on_device(): theirs = lax.ppermute(mine, 'row', swap)  17.4 us
    pallas_call x1, Pallas kernels, unpacked(): pl.pallas_call(functools.partial(unpack_kernel, plan, each), out_shape=(j...  15.3 us
    pallas_call x1, Pallas kernels, ready_rows(): pl.pallas_call(functools.partial(ready_kernel, plan), out_shape=(jax.Shap...  11.5 us
  transfers between devices with their start and end apart: 8, of which 5 were waited for; matrix products, arithmetic and copies ran while one was open for 1% of the time, Pallas kernels for 8%

profile of v3, /device:TPU:69, one launch (start us, length us, event | category | flops | bytes accessed | tf_op | source)
XLA Modules:
  0.0 348.1 jit_solution(17723423892059890655)
XLA Ops:
  7.2 0.1 reduce-scatter.5.cloned.1.call-start
  7.3 0.0 copy-start.5
  7.3 0.0 copy-start.6
  7.3 0.0 copy-start.7
  7.3 22.3 %histograms.1 = (f32[3584,128]{1,0:T(8,128)}, f32[3584,128]{1,0:T(8,128)}) custom-call(s32[1]{0:T(128)} %bitcast.core_ref, s32[10,2048]{1,0:T(8,128)} %bitcast.34, s32[45,2048]{1,0:T(8,128)} %bitcast.33, f32[1,2048]{1,0:T(1,128)} %bitcast.35, f32[1,2048]{1,0:T(1,128)} %bitcast.36), custom_call_target="tpu_custom_call" | custom-call | flops 12000000000 | bytes 8000000 | tf_op jit(solution)/shard_map/histograms/pallas_call | solution.py:165
  29.6 9.9 %collective-permute-start = (f32[3584,128]{1,0:T(8,128)}, f32[3584,128]{1,0:T(8,128)S(1)}, u32[]{:S(2)}, u32[]{:S(2)}) collective-permute-start(f32[3584,128]{1,0:T(8,128)} %get-tuple-element.20), channel_id=1, source_target_pairs={{0,1},{1,0},{2,3},{3,2},{4,5},{5,4},{6,7},{7,6},{8,9},{9,8},{10,11... | collective-permute-start | bytes 5505032 | tf_op jit(solution)/shard_map/ppermute | solution.py:595
  39.5 0.0 copy-done.5
  39.5 0.0 copy-done.6
  39.6 0.2 reshape.49
  39.8 1.0 copy.15
  40.7 0.2 reshape.47
  40.9 1.0 copy.14
  41.9 0.0 copy-done.7
  41.9 0.1 pad_dynamic-slice_fusion.2
  42.0 1.1 collective-permute-done
  43.1 2.9 add.32
  46.0 0.1 reduce-scatter.5.cloned.1.call-update
  46.1 0.1 reduce-scatter.7.cloned.1.call-start
  46.2 0.5 slice_bitcast_fusion
  46.7 9.0 %picked_rows.1 = bf16[32,104,128]{2,1,0:T(8,128)(2,1)} custom-call(s32[12]{0:T(128)} %get-tuple-element.35.terms_ref, s32[160,12]{1,0:T(8,128)} %bitcast.29, s32[160,12]{1,0:T(8,128)} %bitcast.28, bf16[10,200,1024]{2,1,0:T(8,128)(2,1)} %bitcast.20), custom_call_target="tpu_custom_call" | custom-call | flops 1000000000 | bytes 6000000 | tf_op jit(solution)/shard_map/picked_rows/pallas_call | solution.py:227
  55.7 64.5 %all_to_all.15.packet_ref = bf16[32,104,128]{2,1,0:T(8,128)(2,1)} all-to-all(bf16[32,104,128]{2,1,0:T(8,128)(2,1)} %picked_rows.1), channel_id=1, replica_groups=mesh['grp'=4,'row'=32] {'row'}, dimensions={0} | all-to-all | bytes 1703936 | tf_op jit(solution)/shard_map/all_to_all | solution.py:608
  120.2 11.5 %ready_rows.1 = (bf16[12,200,160]{2,1,0:T(8,128)(2,1)}, bf16[12,160,200]{2,1,0:T(8,128)(2,1)}) custom-call(s32[12]{0:T(128)} %get-tuple-element.36.terms_ref, bf16[32,104,128]{2,1,0:T(8,128)(2,1)} %all_to_all.15.packet_ref, bf16[10,200,1024]{2,1,0:T(8,128)(2,1)} %bitcast.21), custom_call_target="tpu_custom_call" | custom-call | flops 1000000000 | bytes 7000000 | tf_op jit(solution)/shard_map/ready_rows/pallas_call | solution.py:343
  131.8 0.0 reduce-scatter.5.cloned.1.call-done.weights_ref
  131.8 0.8 slice.17
  132.5 6.7 %all_to_all.16 = f32[4,16,128]{2,1,0:T(8,128)} all-to-all(f32[4,16,128]{2,1,0:T(8,128)S(1)} %bitcast.30), channel_id=1, replica_groups={{0,32,64,96},{1,33,65,97},{2,34,66,98},{3,35,67,99},{4,36,68,100},{5,37..., dimensions={0} | all-to-all | bytes 65536 | tf_op jit(solution)/shard_map/all_to_all | solution.py:614
  139.2 8.4 %cross_sums.3 = (f32[3840,128]{1,0:T(8,128)}, f32[3840,128]{1,0:T(8,128)}) custom-call(s32[1]{0:T(128)} %bitcast.core_ref, f32[64,128]{1,0:T(8,128)} %bitcast.31, bf16[12,200,160]{2,1,0:T(8,128)(2,1)} %get-tuple-element.24.left_ref, bf16[12,160,200]{2,1,0:T(8,128)(2,1)} %get-tuple-element.25.right_ref), custom_call_target="tpu_custom_call" | custom-call | flops 1000000000 | bytes 6000000 | tf_op jit(solution)/shard_map/cross_sums/pallas_call | solution.py:289
  147.6 8.5 %cross_sums.2 = (f32[3840,128]{1,0:T(8,128)}, f32[3840,128]{1,0:T(8,128)}) custom-call(s32[1]{0:T(128)} %bitcast.core_ref, f32[64,128]{1,0:T(8,128)} %bitcast.32, bf16[12,200,160]{2,1,0:T(8,128)(2,1)} %get-tuple-element.24.left_ref, bf16[12,160,200]{2,1,0:T(8,128)(2,1)} %get-tuple-element.25.right_ref), custom_call_target="tpu_custom_call" | custom-call | flops 1000000000 | bytes 6000000 | tf_op jit(solution)/shard_map/cross_sums/pallas_call | solution.py:289
  156.1 4.6 %collective-permute-start.1 = (f32[3840,128]{1,0:T(8,128)}, f32[3840,128]{1,0:T(8,128)S(1)}, u32[]{:S(2)}, u32[]{:S(2)}) collective-permute-start(f32[3840,128]{1,0:T(8,128)} %get-tuple-element.27), channel_id=1, source_target_pairs={{0,1},{1,0},{2,3},{3,2},{4,5},{5,4},{6,7},{7,6},{8,9},{9,8},{10,11... | collective-permute-start | bytes 5898248 | tf_op jit(solution)/shard_map/ppermute | solution.py:624
  160.7 0.0 collective-permute-start.2
  160.7 8.5 %diag_sums.1 = (f32[1920,128]{1,0:T(8,128)}, f32[1920,128]{1,0:T(8,128)}) custom-call(s32[1]{0:T(128)} %bitcast.core_ref, f32[224,128]{1,0:T(8,128)} %reduce-scatter.5.cloned.1.call-done.weights_ref, bf16[10,200,1024]{2,1,0:T(8,128)(2,1)} %bitcast.22), custom_call_target="tpu_custom_call" | custom-call | flops 1000000000 | bytes 6000000 | tf_op jit(solution)/shard_map/diag_sums/pallas_call | solution.py:289
  169.2 0.5 collective-permute-start.3
  169.7 2.4 collective-permute-done.3.refs_5_
  172.1 0.0 copy-start.4
  172.1 0.0 collective-permute-done.1.refs_1_
  172.1 0.0 copy-start.2
  172.1 0.0 collective-permute-done.2.refs_3_
  172.1 0.9 copy-done.4
  173.1 0.0 copy-start.3
  173.1 0.6 copy-done.2
  173.7 0.6 copy-done.3
  174.3 11.1 %added.1 = f32[9600,128]{1,0:T(8,128)} custom-call(f32[3840,128]{1,0:T(8,128)} %get-tuple-element.26.refs_0_, f32[3840,128]{1,0:T(8,128)} %copy-done.2, f32[3840,128]{1,0:T(8,128)} %get-tuple-element.28.refs_2_, f32[3840,128]{1,0:T(8,128)} %copy-done.3, f32[1920,128]{1,0:T(8,128)} %get-tuple-element.30.refs_4_, f32[1920,128]{1,0:T(8,128)} %copy-done.4), custom_call_target="tpu_custom_call" | custom-call | flops 1000000 | bytes 15000000 | tf_op jit(solution)/shard_map/added/pallas_call | solution.py:436
  185.4 0.1 reduce-scatter.7.cloned.1.call-update
  185.5 67.4 %reduce-scatter.7.cloned.1.call-done.in_ref = f32[600,128]{1,0:T(8,128)} async-done(((f32[9600,128]{1,0:T(8,128)}), f32[600,128]{1,0:T(8,128)}) %reduce-scatter.7.cloned.1.call-update) | async-done | bytes 307216
  252.9 1.8 packed.1
  254.6 1.6 slice.20
  256.2 3.4 all-to-all-start.2
  259.6 0.8 slice.21
  260.4 3.0 all-to-all-done.2
  263.4 39.0 %all-gather.1 = s16[10240,128]{1,0:T(8,128)(2,1)S(1)} all-gather(s16[640,128]{1,0:T(8,128)(2,1)S(1)} %bitcast.27), channel_id=1, replica_groups={{0,2,4,6,8,10,12,14,16,18,20,22,24,26,28,30},{1,3,5,7,9,11,13,15,17,19,..., dimensions={0}, use_global_device_ids=true | all-gather | bytes 2785280 | tf_op jit(solution)/shard_map/all_gather | solution.py:633
  302.4 0.0 copy-start
  302.4 17.4 %collective-permute-start.4 = (s16[10240,128]{1,0:T(8,128)(2,1)S(1)}, s16[10240,128]{1,0:T(8,128)(2,1)S(1)}, u32[]{:S(2)}, u32[]{:S(2)}) collective-permute-start(s16[10240,128]{1,0:T(8,128)(2,1)S(1)} %all-gather.1), channel_id=1, source_target_pairs={{0,1},{1,0},{2,3},{3,2},{4,5},{5,4},{6,7},{7,6},{8,9},{9,8},{10,11... | collective-permute-start | bytes 7864328 | tf_op jit(solution)/shard_map/ppermute | solution.py:636
  319.9 4.5 %collective-permute-done.4 = s16[10240,128]{1,0:T(8,128)(2,1)S(1)} collective-permute-done((s16[10240,128]{1,0:T(8,128)(2,1)S(1)}, s16[10240,128]{1,0:T(8,128)(2,1)S(1)}, u32[]{:S(2)}, u32[]{:S(2)}) %collective-permute-start.4) | collective-permute-done | bytes 2621472 | tf_op jit(solution)/shard_map/ppermute | solution.py:636
  324.4 0.0 copy-start.1
  324.4 1.5 copy-done.1
  325.9 0.0 copy-done
  325.9 15.3 %unpacked.1 = (f32[45,200,200]{2,1,0:T(8,128)}, f32[10,200,200]{2,1,0:T(8,128)}, f32[10,200]{1,0:T(8,128)}) custom-call(s32[1]{0:T(128)} %bitcast.core_ref, s16[16,640,128]{2,1,0:T(8,128)(2,1)} %bitcast.23, s16[16,640,128]{2,1,0:T(8,128)(2,1)} %bitcast.24), custom_call_target="tpu_custom_call" | custom-call | flops 1000000 | bytes 17000000 | tf_op jit(solution)/shard_map/unpacked/pallas_call | solution.py:535
  (3 shorter events, 0.1 us)
Async XLA Ops:
  7.2 124.6 %reduce-scatter.5.cloned.1.call-start = ((), (), s32[]{:S(2)}) async-start(), calls=%async_computation.5 | async-start | bytes 1949696 | tf_op jit(solution)/shard_map/reduce_scatter | solution.py:596
  7.3 32.2 %copy-start.5 = (s32[45,160]{1,0:T(8,128)S(1)}, s32[45,160]{1,0:T(8,128)}, u32[]{:S(2)}) copy-start(s32[45,160]{1,0:T(8,128)} %param.15) | copy-start | bytes 86404
  7.3 32.3 %copy-start.6 = (s32[45,160]{1,0:T(8,128)S(1)}, s32[45,160]{1,0:T(8,128)}, u32[]{:S(2)}) copy-start(s32[45,160]{1,0:T(8,128)} %param.14) | copy-start | bytes 86404
  7.3 34.6 %copy-start.7 = (s32[45,2]{0,1:T(2,128)S(1)}, s32[45,2]{0,1:T(2,128)}, u32[]{:S(2)}) copy-start(s32[45,2]{0,1:T(2,128)} %param.16) | copy-start | bytes 1084
  29.6 13.6 %collective-permute-start = (f32[3584,128]{1,0:T(8,128)}, f32[3584,128]{1,0:T(8,128)S(1)}, u32[]{:S(2)}, u32[]{:S(2)}) collective-permute-start(f32[3584,128]{1,0:T(8,128)} %get-tuple-element.20), channel_id=1, source_target_pairs={{0,1},{1,0},{2,3},{3,2},{4,5},{5,4},{6,7},{7,6},{8,9},{9,8},{10,11... | collective-permute-start | bytes 5505032 | tf_op jit(solution)/shard_map/ppermute | solution.py:595
  46.1 206.8 %reduce-scatter.7.cloned.1.call-start = ((), (), s32[]{:S(2)}) async-start(), calls=%async_computation.6 | async-start | bytes 5222400
  156.1 16.1 %collective-permute-start.1 = (f32[3840,128]{1,0:T(8,128)}, f32[3840,128]{1,0:T(8,128)S(1)}, u32[]{:S(2)}, u32[]{:S(2)}) collective-permute-start(f32[3840,128]{1,0:T(8,128)} %get-tuple-element.27), channel_id=1, source_target_pairs={{0,1},{1,0},{2,3},{3,2},{4,5},{5,4},{6,7},{7,6},{8,9},{9,8},{10,11... | collective-permute-start | bytes 5898248 | tf_op jit(solution)/shard_map/ppermute | solution.py:624
  160.7 11.4 %collective-permute-start.2 = (f32[3840,128]{1,0:T(8,128)}, f32[3840,128]{1,0:T(8,128)S(1)}, u32[]{:S(2)}, u32[]{:S(2)}) collective-permute-start(f32[3840,128]{1,0:T(8,128)} %get-tuple-element.29), channel_id=1, source_target_pairs={{0,1},{1,0},{2,3},{3,2},{4,5},{5,4},{6,7},{7,6},{8,9},{9,8},{10,11... | collective-permute-start | bytes 5898248 | tf_op jit(solution)/shard_map/ppermute | solution.py:624
  169.2 2.9 collective-permute-start.3
  172.1 0.9 copy-start.4
  172.1 1.6 copy-start.2
  173.1 1.3 copy-start.3
  256.2 7.2 %all-to-all-start.2 = ((s16[4,128,128]{2,1,0:T(8,128)(2,1)}), s16[4,128,128]{2,1,0:T(8,128)(2,1)S(1)}, u32[]{:S(2)}, u32[]{:S(2)}) async-start(s16[4,128,128]{2,1,0:T(8,128)(2,1)} %slice.20), calls=%async_computation.3 | async-start | bytes 262144 | tf_op jit(solution)/shard_map/all_to_all | solution.py:628
  302.4 23.5 %copy-start = (s16[10240,128]{1,0:T(8,128)(2,1)}, s16[10240,128]{1,0:T(8,128)(2,1)S(1)}, u32[]{:S(2)}) copy-start(s16[10240,128]{1,0:T(8,128)(2,1)S(1)} %all-gather.1) | copy-start | bytes 7864324
  302.4 22.0 %collective-permute-start.4 = (s16[10240,128]{1,0:T(8,128)(2,1)S(1)}, s16[10240,128]{1,0:T(8,128)(2,1)S(1)}, u32[]{:S(2)}, u32[]{:S(2)}) collective-permute-start(s16[10240,128]{1,0:T(8,128)(2,1)S(1)} %all-gather.1), channel_id=1, source_target_pairs={{0,1},{1,0},{2,3},{3,2},{4,5},{5,4},{6,7},{7,6},{8,9},{9,8},{10,11... | collective-permute-start | bytes 7864328 | tf_op jit(solution)/shard_map/ppermute | solution.py:636
  324.4 1.5 copy-start.1
Sparse Core Ops, SparseCore 0:
  46.2 82.4 reduce-scatter.4
  185.6 67.1 reduce-scatter.6

commit v4 on v3

--- a/solution.py
+++ b/solution.py
@@ -355,10 +355,9 @@
     )(terms, packets, basis)
 
 
-def diag_kernel(plan, core_ref, weights_ref, basis_ref, mine_ref, theirs_ref, work_ref, sums_ref):
-    width, units = plan.width, plan.diag_units
-    blocks = Blocks(plan, core_ref[0], sums_ref, units * UNIT)
-    blocks.clear(plan.covs, units, 0)
+def diag_part(plan, blocks, weights_ref, basis_ref, work_ref):
+    width, units, base = plan.width, plan.diag_units, plan.diag_at
+    blocks.clear(plan.covs, units, base)
     lines = plan.bins // LANES
     work_ref[...] = jnp.zeros_like(work_ref)
     for j in range(plan.covs):
@@ -373,34 +372,24 @@
         rows = weights_ref[pl.ds(pl.multiple_of(j * lines, lines), lines), :]
         weight = jnp.concatenate([rows[t : t + 1] for t in range(lines)], axis=1)
         weighted = (basis.astype(f32) * weight).astype(bf16)
-        blocks.put_square(j, plan.covs, dot(weighted, basis, NT), units, 0)
+        blocks.put_square(j, plan.covs, dot(weighted, basis, NT), units, base)
         return jnp.where(column == j, dot(basis, work, NT), side)
 
     side = lax.fori_loop(0, plan.covs, diag_step, jnp.zeros(column.shape, f32))
     at = plan.covs * plan.tail
     side = jnp.concatenate([side, jnp.zeros((width, LANES - side.shape[1]), f32)], axis=1)
-    blocks.put(plan.diag_blocks - 1, pltpu.roll(side, at, 1), units, 0, at, at + plan.covs)
-    blocks.finish(mine_ref, theirs_ref)
-
-
-def diag_sums(plan, core, weights, basis):
-    work = pltpu.VMEM((up(plan.covs, 16), plan.bins), f32)
-    return sums_call(
-        plan, functools.partial(diag_kernel, plan), "diag_sums", plan.diag_units * UNIT, 10**9,
-        [work], [smem(), vmem(), vmem()], core, weights, basis,
-    )
-
-
-def cross_kernel(plan, first, count, core_ref, pair_w_ref, left_ref, right_ref, mine_ref, theirs_ref, sums_ref):
-    own, units = plan.own, plan.cross_units
-    blocks = Blocks(plan, core_ref[0], sums_ref, count * units * UNIT)
+    blocks.put(plan.diag_blocks - 1, pltpu.roll(side, at, 1), units, base, at, at + plan.covs)
+
+
+def cross_part(plan, blocks, pair_w_ref, left_ref, right_ref):
+    own, units, count = plan.own, plan.cross_units, plan.cluster
     for m in range(count):
         blocks.clear(own, units, m * units * UNIT)
 
     def pair_step(i, carry):
         left, right = left_ref[i].astype(f32), right_ref[i]
         for m in range(count):
-            start = (first + m) * plan.member
+            start = m * plan.member
             turn = (LANES - (i % plan.rest_fold) * plan.rest) % LANES
             rest = pair_w_ref[pl.ds(start + own + i // plan.rest_fold, 1), :]
             rest = pltpu.roll(jnp.broadcast_to(rest, (8, LANES)), turn, 1)[:1, : plan.rest]
@@ -410,39 +399,21 @@
         return carry
 
     lax.fori_loop(0, own, pair_step, 0)
+
+
+def products_kernel(plan, core_ref, weights_ref, pair_w_ref, left_ref, right_ref, basis_ref, mine_ref, theirs_ref, work_ref, sums_ref):
+    blocks = Blocks(plan, core_ref[0], sums_ref, plan.share)
+    diag_part(plan, blocks, weights_ref, basis_ref, work_ref)
+    cross_part(plan, blocks, pair_w_ref, left_ref, right_ref)
     blocks.finish(mine_ref, theirs_ref)
 
 
-def cross_sums(plan, first, count, core, pair_w, left, right):
+def products(plan, core, weights, pair_w, left, right, basis):
+    work = pltpu.VMEM((up(plan.covs, 16), plan.bins), f32)
     return sums_call(
-        plan, functools.partial(cross_kernel, plan, first, count), "cross_sums",
-        count * plan.cross_units * UNIT, 10**9, [], [smem(), vmem(), vmem(), vmem()],
-        core, pair_w, left, right,
+        plan, functools.partial(products_kernel, plan), "products", plan.share, 3 * 10**9,
+        [work], [smem()] + [vmem()] * 5, core, weights, pair_w, left, right, basis,
     )
-
-
-def add_kernel(*refs):
-    out_ref = refs[-1]
-    at = 0
-    for mine_ref, got_ref in zip(refs[:-1:2], refs[1:-1:2]):
-        rows = mine_ref.shape[0]
-        out_ref[at : at + rows, :] = mine_ref[...] + got_ref[...]
-        at += rows
-
-
-def added(plan, parts):
-    flat = [array for pair in parts for array in pair]
-    rows = [array.shape[0] // plan.chips for array in flat]
-    return pl.pallas_call(
-        add_kernel,
-        out_shape=jax.ShapeDtypeStruct((plan.chips * plan.share, LANES), f32),
-        grid=(plan.chips,),
-        in_specs=[pl.BlockSpec((r, LANES), lambda z: (z, 0)) for r in rows],
-        out_specs=pl.BlockSpec((plan.share, LANES), lambda z: (z, 0)),
-        compiler_params=params(),
-        name="added",
-        cost_estimate=pl.CostEstimate(flops=10**6, bytes_accessed=15 * 10**6, transcendentals=0),
-    )(*flat)
 
 
 def pack_kernel(plan, in_ref, out_ref):
@@ -615,13 +586,8 @@
             pair_w.reshape(cluster, plan.member, LANES), "grp", 0, 0,
             axis_index_groups=clusters, tiled=True,
         ).reshape(cluster * plan.member, LANES)
-    diag = diag_sums(plan, core, sums, basis)
-    step = -(-cluster // 2)
-    parts = [
-        cross_sums(plan, first, min(step, cluster - first), core, pair_w, left, right)
-        for first in range(0, cluster, step)
-    ] + [diag]
-    total = added(plan, [(mine, lax.ppermute(theirs, "row", swap)) for mine, theirs in parts])
+    mine, theirs = products(plan, core, sums, pair_w, left, right, basis)
+    total = mine + lax.ppermute(theirs, "row", swap)
     total = lax.psum_scatter(total, "row", axis_index_groups=rings, tiled=True)
     chunks = packed(plan, total)
     if cluster > 1:

time: 350 us -> 338 us (0.966)
  Pallas kernels: 96.4 us -> 78.3 us
  waiting for transfers between devices: 78.6 us -> 83.9 us
  other arithmetic: 2.94 us -> 7.24 us
    pallas_call x1 -> x0, Pallas kernels: 11.1 us -> none  [added(): pl.pallas_call(add_kernel, out_shape=jax.ShapeDtypeStruct((plan.chips * p...]
    pallas_call x3 -> x1, Pallas kernels: 25.4 us -> 18.4 us  [sums_call(): pl.pallas_call(kernel, out_shape=(out, out), in_specs=ins, out_specs=(vme...]
    ppermute x3 -> x1, waiting for transfers between devices: 2.41 us -> 8.03 us  [on_device(): total = mine + lax.ppermute(theirs, 'row', swap)]
    add x0 -> x1, other arithmetic: none -> 4.29 us  [on_device(): total = mine + lax.ppermute(theirs, 'row', swap)]
  transfers between devices with their start and end apart: 8 -> 6, of which waited for: 5 -> 5; matrix products, arithmetic and copies ran while one was open for 1% -> 1% of each run, Pallas kernels for 8% -> 6%
where the time goes in v4:
time: 338 us
  blocking collectives  111 us (33%)
  waiting for transfers between devices  83.9 us (25%)
  Pallas kernels  78.3 us (23%)
  starting transfers between devices  35.9 us (11%)
  between operations  14.2 us (4%)
  local copies, waits for them, and re-layouts  7.63 us (2%)
  other arithmetic  7.24 us (2%)
    unnamed x3, waiting for transfers between devices  67.2 us
    all_to_all x1, blocking collectives, on_device(): lax.all_to_all(packets, 'row', split_axis=0, concat_axis=0, tiled=True)  64.6 us
    all_gather x1, blocking collectives, on_device(): lax.all_gather(chunks.reshape(length, LANES), 'row', axis=0, axis_index_g...  39.2 us
    pallas_call x1, Pallas kernels, histograms(): pl.pallas_call(functools.partial(hist_kernel, plan), out_shape=(out, out)...  22.3 us
    pallas_call x1, Pallas kernels, sums_call(): pl.pallas_call(kernel, out_shape=(out, out), in_specs=ins, out_specs=(vme...  18.4 us
    ppermute x1, starting transfers between devices, on_device(): theirs = lax.ppermute(mine, 'row', swap)  17.9 us
    pallas_call x1, Pallas kernels, unpacked(): pl.pallas_call(functools.partial(unpack_kernel, plan, each), out_shape=(j...  15.3 us
    pallas_call x1, Pallas kernels, ready_rows(): pl.pallas_call(functools.partial(ready_kernel, plan), out_shape=(jax.Shap...  11.6 us
  transfers between devices with their start and end apart: 6, of which 5 were waited for; matrix products, arithmetic and copies ran while one was open for 1% of the time, Pallas kernels for 6%

profile of v4, /device:TPU:69, one launch (start us, length us, event | category | flops | bytes accessed | tf_op | source)
XLA Modules:
  0.0 337.7 jit_solution(17210330713402365584)
XLA Ops:
  7.2 0.1 reduce-scatter.5.cloned.1.call-start
  7.3 0.0 copy-start.2
  7.3 0.0 copy-start.3
  7.3 0.0 copy-start.4
  7.3 22.3 %histograms.1 = (f32[3584,128]{1,0:T(8,128)}, f32[3584,128]{1,0:T(8,128)}) custom-call(s32[1]{0:T(128)} %bitcast.core_ref, s32[10,2048]{1,0:T(8,128)} %bitcast.33, s32[45,2048]{1,0:T(8,128)} %bitcast.32, f32[1,2048]{1,0:T(1,128)} %bitcast.34, f32[1,2048]{1,0:T(1,128)} %bitcast.35), custom_call_target="tpu_custom_call" | custom-call | flops 12000000000 | bytes 8000000 | tf_op jit(solution)/shard_map/histograms/pallas_call | solution.py:165
  29.6 9.9 %collective-permute-start = (f32[3584,128]{1,0:T(8,128)}, f32[3584,128]{1,0:T(8,128)S(1)}, u32[]{:S(2)}, u32[]{:S(2)}) collective-permute-start(f32[3584,128]{1,0:T(8,128)} %get-tuple-element.16), channel_id=1, source_target_pairs={{0,1},{1,0},{2,3},{3,2},{4,5},{5,4},{6,7},{7,6},{8,9},{9,8},{10,11... | collective-permute-start | bytes 5505032 | tf_op jit(solution)/shard_map/ppermute | solution.py:566
  39.5 0.0 copy-done.2
  39.5 0.0 copy-done.3
  39.6 0.2 reshape.49
  39.8 1.0 copy.15
  40.8 0.2 reshape.47
  41.0 1.0 copy.14
  41.9 0.0 copy-done.4
  41.9 0.1 pad_dynamic-slice_fusion.2
  42.0 1.1 collective-permute-done
  43.1 2.9 add.35
  46.0 0.1 reduce-scatter.5.cloned.1.call-update
  46.1 0.1 reduce-scatter.7.cloned.1.call-start
  46.2 0.6 slice_bitcast_fusion
  46.7 9.0 %picked_rows.1 = bf16[32,104,128]{2,1,0:T(8,128)(2,1)} custom-call(s32[12]{0:T(128)} %get-tuple-element.27.terms_ref, s32[160,12]{1,0:T(8,128)} %bitcast.29, s32[160,12]{1,0:T(8,128)} %bitcast.28, bf16[10,200,1024]{2,1,0:T(8,128)(2,1)} %bitcast.20), custom_call_target="tpu_custom_call" | custom-call | flops 1000000000 | bytes 6000000 | tf_op jit(solution)/shard_map/picked_rows/pallas_call | solution.py:227
  55.8 64.6 %all_to_all.15.packet_ref = bf16[32,104,128]{2,1,0:T(8,128)(2,1)} all-to-all(bf16[32,104,128]{2,1,0:T(8,128)(2,1)} %picked_rows.1), channel_id=1, replica_groups=mesh['grp'=4,'row'=32] {'row'}, dimensions={0} | all-to-all | bytes 1703936 | tf_op jit(solution)/shard_map/all_to_all | solution.py:579
  120.3 11.6 %ready_rows.1 = (bf16[12,200,160]{2,1,0:T(8,128)(2,1)}, bf16[12,160,200]{2,1,0:T(8,128)(2,1)}) custom-call(s32[12]{0:T(128)} %get-tuple-element.28.terms_ref, bf16[32,104,128]{2,1,0:T(8,128)(2,1)} %all_to_all.15.packet_ref, bf16[10,200,1024]{2,1,0:T(8,128)(2,1)} %bitcast.21), custom_call_target="tpu_custom_call" | custom-call | flops 1000000000 | bytes 7000000 | tf_op jit(solution)/shard_map/ready_rows/pallas_call | solution.py:343
  131.9 0.0 reduce-scatter.5.cloned.1.call-done.weights_ref
  131.9 0.8 slice.17
  132.7 6.7 %all_to_all.16 = f32[4,16,128]{2,1,0:T(8,128)} all-to-all(f32[4,16,128]{2,1,0:T(8,128)S(1)} %bitcast.30), channel_id=1, replica_groups={{0,32,64,96},{1,33,65,97},{2,34,66,98},{3,35,67,99},{4,36,68,100},{5,37..., dimensions={0} | all-to-all | bytes 65536 | tf_op jit(solution)/shard_map/all_to_all | solution.py:585
  139.3 18.4 %products.1 = (f32[9600,128]{1,0:T(8,128)}, f32[9600,128]{1,0:T(8,128)}) custom-call(s32[1]{0:T(128)} %bitcast.core_ref, f32[224,128]{1,0:T(8,128)} %reduce-scatter.5.cloned.1.call-done.weights_ref, f32[64,128]{1,0:T(8,128)} %bitcast.31, bf16[12,200,160]{2,1,0:T(8,128)(2,1)} %get-tuple-element.20.left_ref, ...), custom_call_target="tpu_custom_call" | custom-call | flops 3000000000 | bytes 6000000 | tf_op jit(solution)/shard_map/products/pallas_call | solution.py:289
  157.7 4.6 %collective-permute-start.1 = (f32[9600,128]{1,0:T(8,128)}, f32[9600,128]{1,0:T(8,128)S(1)}, u32[]{:S(2)}, u32[]{:S(2)}) collective-permute-start(f32[9600,128]{1,0:T(8,128)} %get-tuple-element.23), channel_id=1, source_target_pairs={{0,1},{1,0},{2,3},{3,2},{4,5},{5,4},{6,7},{7,6},{8,9},{9,8},{10,11... | collective-permute-start | bytes 14745608 | tf_op jit(solution)/shard_map/ppermute | solution.py:590
  162.3 8.0 %collective-permute-done.1 = f32[9600,128]{1,0:T(8,128)S(1)} collective-permute-done((f32[9600,128]{1,0:T(8,128)}, f32[9600,128]{1,0:T(8,128)S(1)}, u32[]{:S(2)}, u32[]{:S(2)}) %collective-permute-start.1) | collective-permute-done | bytes 4915232 | tf_op jit(solution)/shard_map/ppermute | solution.py:590
  170.3 4.3 %add.39 = f32[9600,128]{1,0:T(8,128)} add(f32[9600,128]{1,0:T(8,128)} %get-tuple-element.22, f32[9600,128]{1,0:T(8,128)S(1)} %collective-permute-done.1) | non-fusion elementwise | flops 1228800 | bytes 14745600 | tf_op jit(solution)/shard_map/add | solution.py:590
  174.6 0.1 reduce-scatter.7.cloned.1.call-update
  174.7 67.1 %reduce-scatter.7.cloned.1.call-done.in_ref = f32[600,128]{1,0:T(8,128)} async-done(((f32[9600,128]{1,0:T(8,128)}), f32[600,128]{1,0:T(8,128)}) %reduce-scatter.7.cloned.1.call-update) | async-done | bytes 307216
  241.8 1.8 packed.1
  243.6 1.6 slice.20
  245.1 3.4 %all-to-all-start.2 = ((s16[4,128,128]{2,1,0:T(8,128)(2,1)}), s16[4,128,128]{2,1,0:T(8,128)(2,1)S(1)}, u32[]{:S(2)}, u32[]{:S(2)}) async-start(s16[4,128,128]{2,1,0:T(8,128)(2,1)} %slice.20), calls=%async_computation.3 | async-start | bytes 262144 | tf_op jit(solution)/shard_map/all_to_all | solution.py:594
  248.6 0.8 slice.21
  249.3 3.0 all-to-all-done.2
  252.4 39.2 %all-gather.1 = s16[10240,128]{1,0:T(8,128)(2,1)S(1)} all-gather(s16[640,128]{1,0:T(8,128)(2,1)S(1)} %bitcast.27), channel_id=1, replica_groups={{0,2,4,6,8,10,12,14,16,18,20,22,24,26,28,30},{1,3,5,7,9,11,13,15,17,19,..., dimensions={0}, use_global_device_ids=true | all-gather | bytes 2785280 | tf_op jit(solution)/shard_map/all_gather | solution.py:599
  291.6 0.0 copy-start
  291.6 17.9 %collective-permute-start.2 = (s16[10240,128]{1,0:T(8,128)(2,1)S(1)}, s16[10240,128]{1,0:T(8,128)(2,1)S(1)}, u32[]{:S(2)}, u32[]{:S(2)}) collective-permute-start(s16[10240,128]{1,0:T(8,128)(2,1)S(1)} %all-gather.1), channel_id=1, source_target_pairs={{0,1},{1,0},{2,3},{3,2},{4,5},{5,4},{6,7},{7,6},{8,9},{9,8},{10,11... | collective-permute-start | bytes 7864328 | tf_op jit(solution)/shard_map/ppermute | solution.py:602
  309.5 4.5 %collective-permute-done.2 = s16[10240,128]{1,0:T(8,128)(2,1)S(1)} collective-permute-done((s16[10240,128]{1,0:T(8,128)(2,1)S(1)}, s16[10240,128]{1,0:T(8,128)(2,1)S(1)}, u32[]{:S(2)}, u32[]{:S(2)}) %collective-permute-start.2) | collective-permute-done | bytes 2621472 | tf_op jit(solution)/shard_map/ppermute | solution.py:602
  314.0 0.0 copy-start.1
  314.0 1.5 copy-done.1
  315.5 0.0 copy-done
  315.5 15.3 %unpacked.1 = (f32[45,200,200]{2,1,0:T(8,128)}, f32[10,200,200]{2,1,0:T(8,128)}, f32[10,200]{1,0:T(8,128)}) custom-call(s32[1]{0:T(128)} %bitcast.core_ref, s16[16,640,128]{2,1,0:T(8,128)(2,1)} %bitcast.23, s16[16,640,128]{2,1,0:T(8,128)(2,1)} %bitcast.24), custom_call_target="tpu_custom_call" | custom-call | flops 1000000 | bytes 17000000 | tf_op jit(solution)/shard_map/unpacked/pallas_call | solution.py:506
  (3 shorter events, 0.1 us)
Async XLA Ops:
  7.2 124.7 %reduce-scatter.5.cloned.1.call-start = ((), (), s32[]{:S(2)}) async-start(), calls=%async_computation.5 | async-start | bytes 1949696 | tf_op jit(solution)/shard_map/reduce_scatter | solution.py:567
  7.3 32.2 %copy-start.2 = (s32[45,160]{1,0:T(8,128)S(1)}, s32[45,160]{1,0:T(8,128)}, u32[]{:S(2)}) copy-start(s32[45,160]{1,0:T(8,128)} %param.15) | copy-start | bytes 86404
  7.3 32.3 %copy-start.3 = (s32[45,160]{1,0:T(8,128)S(1)}, s32[45,160]{1,0:T(8,128)}, u32[]{:S(2)}) copy-start(s32[45,160]{1,0:T(8,128)} %param.14) | copy-start | bytes 86404
  7.3 34.7 %copy-start.4 = (s32[45,2]{0,1:T(2,128)S(1)}, s32[45,2]{0,1:T(2,128)}, u32[]{:S(2)}) copy-start(s32[45,2]{0,1:T(2,128)} %param.16) | copy-start | bytes 1084
  29.6 13.6 %collective-permute-start = (f32[3584,128]{1,0:T(8,128)}, f32[3584,128]{1,0:T(8,128)S(1)}, u32[]{:S(2)}, u32[]{:S(2)}) collective-permute-start(f32[3584,128]{1,0:T(8,128)} %get-tuple-element.16), channel_id=1, source_target_pairs={{0,1},{1,0},{2,3},{3,2},{4,5},{5,4},{6,7},{7,6},{8,9},{9,8},{10,11... | collective-permute-start | bytes 5505032 | tf_op jit(solution)/shard_map/ppermute | solution.py:566
  46.1 195.7 %reduce-scatter.7.cloned.1.call-start = ((), (), s32[]{:S(2)}) async-start(), calls=%async_computation.6 | async-start | bytes 5222400
  157.7 12.6 %collective-permute-start.1 = (f32[9600,128]{1,0:T(8,128)}, f32[9600,128]{1,0:T(8,128)S(1)}, u32[]{:S(2)}, u32[]{:S(2)}) collective-permute-start(f32[9600,128]{1,0:T(8,128)} %get-tuple-element.23), channel_id=1, source_target_pairs={{0,1},{1,0},{2,3},{3,2},{4,5},{5,4},{6,7},{7,6},{8,9},{9,8},{10,11... | collective-permute-start | bytes 14745608 | tf_op jit(solution)/shard_map/ppermute | solution.py:590
  245.1 7.2 %all-to-all-start.2 = ((s16[4,128,128]{2,1,0:T(8,128)(2,1)}), s16[4,128,128]{2,1,0:T(8,128)(2,1)S(1)}, u32[]{:S(2)}, u32[]{:S(2)}) async-start(s16[4,128,128]{2,1,0:T(8,128)(2,1)} %slice.20), calls=%async_computation.3 | async-start | bytes 262144 | tf_op jit(solution)/shard_map/all_to_all | solution.py:594
  291.6 23.9 %copy-start = (s16[10240,128]{1,0:T(8,128)(2,1)}, s16[10240,128]{1,0:T(8,128)(2,1)S(1)}, u32[]{:S(2)}) copy-start(s16[10240,128]{1,0:T(8,128)(2,1)S(1)} %all-gather.1) | copy-start | bytes 7864324
  291.6 22.4 %collective-permute-start.2 = (s16[10240,128]{1,0:T(8,128)(2,1)S(1)}, s16[10240,128]{1,0:T(8,128)(2,1)S(1)}, u32[]{:S(2)}, u32[]{:S(2)}) collective-permute-start(s16[10240,128]{1,0:T(8,128)(2,1)S(1)} %all-gather.1), channel_id=1, source_target_pairs={{0,1},{1,0},{2,3},{3,2},{4,5},{5,4},{6,7},{7,6},{8,9},{9,8},{10,11... | collective-permute-start | bytes 7864328 | tf_op jit(solution)/shard_map/ppermute | solution.py:602
  314.0 1.5 copy-start.1
Sparse Core Ops, SparseCore 0:
  46.2 81.6 reduce-scatter.4
  174.8 66.9 reduce-scatter.6
